TPU v7x, 32 devices: a whole 2x2x4 slice. The times are simulated.
32 devices in a mesh: texel: 8 (over y, x, core), light: 4 (over z).
Axes of the slice: x: 2, y: 2, z: 4, core: 2. Of those that a mesh axis runs over, the one named last changes fastest.
Arguments:
- tex_feat: bfloat16 [8192, 512], P('texel'), may hold values from -18 to 18
- light_feat: bfloat16 [6144, 512], P('light'), may hold values from -0.25 to 0.25
- sketch: bfloat16 [6144, 256], P('light'), may hold values from -0.078125 to 0.078125
- row_counts: int32 [8], replicated, may hold values from 1 to 1024, 4096 in all
Outputs:
- basis: float32 [8192, 256], P('texel')
- coeffs: float32 [256, 6144], P('texel', 'light')
Inputs may be any that keep to these rules, and one draw needn't show every extreme that they name: row_counts sums to 8 * 512; some entry equals 1024.
All inputs are finite; a program needn't handle non-finite values.
Results may differ from a plain program's by a relative error of at most 0.0034.
Values sent between devices are 32-bit elements; how exact they have to be, the bound alone decides.
A program may use at most 64 MiB of HBM per device.

v0:
```python
import functools

import jax
import jax.numpy as jnp
from jax import lax
from jax.experimental import pallas as pl
from jax.experimental.pallas import tpu as pltpu
from jax.sharding import PartitionSpec as P

HIGHEST = lax.Precision.HIGHEST
BLOCK = 64
INV_TWO_PI = 0.15915494309189535
TWO_PI_HIGH = 6.28125
TWO_PI_LOW = 0.001935307179586232
SINE = (
    0.9999999944783076,
    -0.16666664569596037,
    0.008333310280569169,
    -0.00019840151040396647,
    2.752937413742719e-06,
    -2.4676261406891767e-08,
    1.344908473337278e-10,
)


def bounded_sine(x):
    turns = jnp.round(x * INV_TWO_PI)
    r = (x - turns * TWO_PI_HIGH) - turns * TWO_PI_LOW
    s = r * r
    value = jnp.full_like(s, SINE[-1])
    for coefficient in SINE[-2::-1]:
        value = value * s + coefficient
    return value * r


def eliminate(block):
    rows = [block[8 * t : 8 * t + 8, :] for t in range(8)]
    below = lax.broadcasted_iota(jnp.int32, (8, 128), 0)
    for p in range(8):
        columns = {
            (t, k): jnp.broadcast_to(rows[t][:, 8 * p + k : 8 * p + k + 1], (8, 128))
            for t in range(p, 8)
            for k in range(8)
        }
        for k in range(8):
            inverse = 1.0 / jnp.broadcast_to(columns[p, k][k : k + 1, :], (8, 128))
            pivot_row = jnp.broadcast_to(rows[p][k : k + 1, :], (8, 128))
            entries = [
                jnp.broadcast_to(columns[p, later][k : k + 1, :], (8, 128))
                for later in range(k + 1, 8)
            ]
            for t in range(p, 8):
                factor = columns[t, k] * inverse
                if t == p:
                    factor = jnp.where(below > k, factor, 0.0)
                rows[t] = rows[t] - factor * pivot_row
                for later in range(k + 1, 8):
                    columns[t, later] = columns[t, later] - factor * entries[later - k - 1]
    return jnp.concatenate(rows, axis=0)


def factor_inverse(gram_ref, inverse_ref, work_ref):
    size = gram_ref.shape[0]
    work_ref[...] = gram_ref[...]
    row = lax.broadcasted_iota(jnp.int32, (size, size), 0)
    column = lax.broadcasted_iota(jnp.int32, (size, size), 1)
    inverse_ref[...] = jnp.where(row == column, 1.0, 0.0).astype(jnp.float32)
    lane = lax.broadcasted_iota(jnp.int32, (BLOCK, 128), 1)
    line = lax.broadcasted_iota(jnp.int32, (BLOCK, 128), 0)
    for start in range(0, size, BLOCK):
        own = slice(start, start + BLOCK)
        tile_start = start // 128 * 128
        tile = work_ref[own, tile_start : tile_start + 128]
        if start % 128:
            tile = pltpu.roll(tile, 64, 1)
        unit = jnp.where(lane - BLOCK == line, 1.0, 0.0)
        done = eliminate(jnp.where(lane < BLOCK, tile, unit))
        pivots = jnp.sum(jnp.where(lane == line, done, 0.0), axis=1, keepdims=True)
        scaled = pltpu.roll(done * lax.rsqrt(pivots), 64, 1)[:, :BLOCK]
        left = jnp.dot(scaled, work_ref[own, :], precision=HIGHEST, preferred_element_type=jnp.float32)
        right = jnp.dot(scaled, inverse_ref[own, :], precision=HIGHEST, preferred_element_type=jnp.float32)
        inverse_ref[own, :] = right
        rest = size - start - BLOCK
        if rest:
            lower = slice(start + BLOCK, size)
            flipped = left.T[start + BLOCK :, :]
            work_ref[lower, :] -= jnp.dot(flipped, left, precision=HIGHEST, preferred_element_type=jnp.float32)
            inverse_ref[lower, :] -= jnp.dot(flipped, right, precision=HIGHEST, preferred_element_type=jnp.float32)


MESH_ID = pl.DeviceIdType.MESH


def greet(peers):
    barrier = pltpu.get_barrier_semaphore()
    for peer in peers:
        pl.semaphore_signal(barrier, inc=1, device_id=peer, device_id_type=MESH_ID)
    pl.semaphore_wait(barrier, len(peers))


def sketch_and_gram(
    n_texel, n_light, tex_ref, feat_ref, sketch_ref, used_ref, count_ref, whole_ref, inverse_ref, tile_ref,
    logits, partial_ref,
    landed, whole, pieces, plane, column, gram, scaled, work,
    part_send, part_recv, plane_send, plane_recv, column_send, column_recv,
    full_send, full_recv, row_send, row_recv,
):
    texel, light = lax.axis_index("texel"), lax.axis_index("light")
    depth = partial_ref.shape[0] // n_light
    size = partial_ref.shape[1]
    piece = size // n_texel
    lights = [lax.rem(light + d, n_light) for d in range(n_light)]
    texels = [lax.rem(texel + d, n_texel) for d in range(n_texel)]
    greet([(texel, lights[d]) for d in range(1, n_light)] + [(texels[d], light) for d in range(1, n_texel)])

    def send(source, target, send_sem, recv_sem, device):
        copy = pltpu.make_async_remote_copy(
            src_ref=source, dst_ref=target, send_sem=send_sem, recv_sem=recv_sem,
            device_id=device, device_id_type=MESH_ID,
        )
        copy.start()
        return copy

    def rows_of(index, height):
        return pl.ds(pl.multiple_of(index * height, height), height)

    step = logits.shape[1]

    def fill(index):
        texels_here = tex_ref[rows_of(index, depth), :]

        def block(c, carry):
            columns = rows_of(c, step)
            logits[...] = lax.dot_general(
                texels_here, feat_ref[columns, :], (((1,), (1,)), ((), ())), preferred_element_type=jnp.float32
            )

            def strip(i, inner):
                value = bounded_sine(logits[rows_of(i, 16), :]).astype(jnp.bfloat16)
                tile_ref[pl.ds(pl.multiple_of(index * depth + i * 16, 16), 16), columns] = value
                return inner

            return lax.fori_loop(0, depth // 16, strip, carry, unroll=2)

        lax.fori_loop(0, feat_ref.shape[0] // step, block, 0)
        rows = rows_of(index, depth)
        partial_ref[rows, :] = (
            jnp.dot(tile_ref[rows, :], sketch_ref[...], preferred_element_type=jnp.float32) * used_ref[rows, :]
        )

    copies = []
    for d in range(1, n_light):
        fill(lights[d])
        copies.append(
            send(
                partial_ref.at[rows_of(lights[d], depth)], landed.at[d],
                part_send.at[d], part_recv.at[d], (texel, lights[d]),
            )
        )
    fill(light)
    own = partial_ref[rows_of(light, depth), :]
    for d, copy in enumerate(copies, 1):
        copy.wait()
        own = own + landed[d]
    whole[rows_of(light, depth), :] = own
    early = depth // 4

    def gather(part, first, height):
        rows = pl.ds(pl.multiple_of(light * depth + first, 8), height)
        return [
            send(
                whole.at[rows], whole.at[rows], full_send.at[part, d], full_recv.at[part, d], (texel, lights[d])
            )
            for d in range(1, n_light)
        ]

    gathers = gather(0, 0, early)
    local = lax.dot_general(
        own, own, (((0,), (0,)), ((), ())), precision=HIGHEST, preferred_element_type=jnp.float32
    )
    for index in range(n_texel):
        pieces[index] = local[index * piece : (index + 1) * piece, :]
    copies = [
        send(pieces.at[texels[d]], plane.at[d], plane_send.at[d], plane_recv.at[d], (texels[d], light))
        for d in range(1, n_texel)
    ]
    total = pieces[texel]
    for d, copy in enumerate(copies, 1):
        copy.wait()
        total = total + plane[d]
    column[light] = total
    copies = [
        send(column.at[light], column.at[light], column_send.at[d], column_recv.at[d], (texel, lights[d]))
        for d in range(1, n_light)
    ]
    for copy in copies:
        copy.wait()
    gathers += gather(1, early, depth - early)
    total = column[0]
    for index in range(1, n_light):
        total = total + column[index]
    gram[rows_of(texel, piece), :] = total
    copies = [
        send(
            gram.at[rows_of(texel, piece)], gram.at[rows_of(texel, piece)],
            row_send.at[d], row_recv.at[d], (texels[d], light),
        )
        for d in range(1, n_texel)
    ]
    for copy in copies:
        copy.wait()
    scaled[...] = gram[...] / count_ref[...]
    factor_inverse(scaled, inverse_ref, work)
    for copy in gathers:
        copy.wait()
    whole_ref[...] = whole[...]


def reduced(tex_feat, light_feat, sketch, used, count, n_texel, n_light):
    capacity, size = tex_feat.shape[0], sketch.shape[1]
    lights = light_feat.shape[0]
    step = next(w for w in (512, 256, 128) if lights % w == 0)
    depth, piece = capacity // n_light, size // n_texel
    vmem = pl.BlockSpec(memory_space=pltpu.VMEM)
    f32 = jnp.float32
    sems = pltpu.SemaphoreType.DMA
    return pl.pallas_call(
        functools.partial(sketch_and_gram, n_texel, n_light),
        out_shape=(
            jax.ShapeDtypeStruct((capacity, size), f32),
            jax.ShapeDtypeStruct((size, size), f32),
            jax.ShapeDtypeStruct((capacity, lights), jnp.bfloat16),
        ),
        in_specs=[vmem] * 5,
        out_specs=(vmem, vmem, vmem),
        scratch_shapes=[
            pltpu.VMEM((depth, step), f32),
            pltpu.VMEM((capacity, size), f32),
            pltpu.VMEM((n_light, depth, size), f32),
            pltpu.VMEM((capacity, size), f32),
            pltpu.VMEM((n_texel, piece, size), f32),
            pltpu.VMEM((n_texel, piece, size), f32),
            pltpu.VMEM((n_light, piece, size), f32),
            pltpu.VMEM((size, size), f32),
            pltpu.VMEM((size, size), f32),
            pltpu.VMEM((size, size), f32),
            sems((n_light,)), sems((n_light,)),
            sems((n_texel,)), sems((n_texel,)),
            sems((n_light,)), sems((n_light,)),
            sems((2, n_light)), sems((2, n_light)),
            sems((n_texel,)), sems((n_texel,)),
        ],
        compiler_params=pltpu.CompilerParams(collective_id=1, has_side_effects=True),
    )(tex_feat, light_feat, sketch, used, count)


def halving_order(bits, last_first):
    rest = list(range(1, bits))
    return [0] + (rest[::-1] if last_first else rest)


def scatter_sum(n_texel, partial_ref, out_ref, held, landed, send_sem, recv_sem):
    texel, light = lax.axis_index("texel"), lax.axis_index("light")
    bits = n_texel.bit_length() - 1
    bit = [lax.rem(texel // (1 << b), 2) for b in range(bits)]
    partner = [texel + (1 - 2 * bit[b]) * (1 << b) for b in range(bits)]
    greet([(partner[b], light) for b in range(bits)])
    piece = partial_ref.shape[0] // n_texel
    width = partial_ref.shape[1] // 2

    def start_of(mask):
        block = 0
        for b in range(bits):
            flipped = 1 - bit[b] if mask >> b & 1 else bit[b]
            block = block + flipped * (1 << b)
        return pl.multiple_of(block * piece, piece)

    orders = [halving_order(bits, False), halving_order(bits, True)]
    flights = [{}, {}]
    for step in range(bits):
        for half, order in enumerate(orders):
            b = order[step]
            left = [m for m in range(n_texel) if all(not m >> done & 1 for done in order[:step])]
            later = order[step + 1 :]
            going = [m for m in left if m >> b & 1]
            going.sort(key=lambda m: [-(m >> c & 1) for c in later])
            columns = pl.ds(half * width, width)
            for m in going:
                kept = m - (1 << b)
                if step == 0:
                    source = partial_ref.at[pl.ds(start_of(m), piece), columns]
                else:
                    arrived = flights[half].pop((step - 1, m))
                    arrived.wait()
                    below = (
                        partial_ref[pl.ds(start_of(m), piece), columns] if step == 1 else held[half, m]
                    )
                    held[half, m] = below + landed[half, step - 1, m]
                    source = held.at[half, m]
                copy = pltpu.make_async_remote_copy(
                    src_ref=source,
                    dst_ref=landed.at[half, step, kept],
                    send_sem=send_sem.at[half, step, kept],
                    recv_sem=recv_sem.at[half, step, kept],
                    device_id=(partner[b], light),
                    device_id_type=MESH_ID,
                )
                copy.start()
                flights[half][step, kept] = copy
        if step:
            for half, order in enumerate(orders):
                for key in [k for k in flights[half] if k[0] == step - 1]:
                    m = key[1]
                    flights[half].pop(key).wait()
                    columns = pl.ds(half * width, width)
                    below = (
                        partial_ref[pl.ds(start_of(m), piece), columns] if step == 1 else held[half, m]
                    )
                    held[half, m] = below + landed[half, step - 1, m]
    for half in range(2):
        columns = pl.ds(half * width, width)
        flights[half].pop((bits - 1, 0)).wait()
        below = partial_ref[pl.ds(start_of(0), piece), columns] if bits == 1 else held[half, 0]
        out_ref[:, half * width : (half + 1) * width] = below + landed[half, bits - 1, 0]


def scattered(partial, n_texel):
    size, lights = partial.shape
    piece, width, bits = size // n_texel, lights // 2, n_texel.bit_length() - 1
    vmem = pl.BlockSpec(memory_space=pltpu.VMEM)
    return pl.pallas_call(
        functools.partial(scatter_sum, n_texel),
        out_shape=jax.ShapeDtypeStruct((piece, lights), jnp.float32),
        in_specs=[vmem],
        out_specs=vmem,
        scratch_shapes=[
            pltpu.VMEM((2, n_texel, piece, width), jnp.float32),
            pltpu.VMEM((2, bits, n_texel, piece, width), jnp.float32),
            pltpu.SemaphoreType.DMA((2, bits, n_texel)),
            pltpu.SemaphoreType.DMA((2, bits, n_texel)),
        ],
        compiler_params=pltpu.CompilerParams(collective_id=2, has_side_effects=True),
    )(partial)


def on_device(n_texel, n_light, tex_feat, light_feat, sketch, row_counts):
    capacity = tex_feat.shape[0]
    own_count = row_counts[lax.axis_index("texel")]
    valid_total = jnp.sum(row_counts).astype(jnp.float32)
    row_valid = (lax.iota(jnp.int32, capacity) < own_count).astype(jnp.float32)
    count = jnp.full((1, sketch.shape[1]), valid_total)
    sketched, inverse, tile_block = reduced(
        tex_feat, light_feat, sketch, row_valid[:, None], count, n_texel, n_light
    )
    basis = lax.dot_general(sketched, inverse, (((1,), (1,)), ((), ())), precision=HIGHEST)
    basis_half = basis.astype(jnp.bfloat16)
    partial_coeffs = lax.dot_general(
        basis_half, tile_block, (((0,), (0,)), ((), ())), preferred_element_type=jnp.float32
    )
    coeffs = scattered(partial_coeffs, n_texel) / jnp.sqrt(valid_total)
    return (basis, coeffs)


def solution(mesh):
    placed = (P("texel", None), P("light", None), P("light", None), P())
    return jax.shard_map(
        functools.partial(on_device, mesh.shape["texel"], mesh.shape["light"]),
        mesh=mesh,
        in_specs=placed,
        out_specs=(P("texel", None), P("texel", "light")),
        check_vma=False,
    )
```

profile of v0, /device:TPU:24, one launch (start us, length us, event | category | flops | bytes accessed | tf_op | source)
XLA Modules:
  0.0 92.9 jit_solution(9944441451946981493)
XLA Ops:
  0.6 1.3 %reduce_sum.9 = s32[]{:T(128)} reduce(s32[8]{0:T(128)} %param.7, s32[]{:T(128)} %constant.8.clone.1), dimensions={0}, to_apply=%region_0.0 | reduce | flops 7 | bytes 40 | tf_op jit(solution)/shard_map/reduce_sum | solution.py:349
  2.6 1.3 %dynamic_slice.3 = s32[1]{0:T(128)} dynamic-slice(s32[8]{0:T(128)} %param.7, s32[]{:T(128)S(6)} %select_n.3), dynamic_slice_sizes={1} | dynamic-slice | bytes 12 | tf_op jit(solution)/shard_map/dynamic_slice | solution.py:348
  3.9 0.6 broadcast_in_dim.4.count_ref
  4.5 1.5 %fusion.2.used_ref = f32[1024,1]{1,0:T(8,128)} fusion(s32[]{:T(128)} %bitcast), kind=kLoop, calls=%fused_computation.3 | loop fusion | flops 2048 | bytes 4100 | tf_op jit(solution)/shard_map/convert_element_type | solution.py:350
  6.0 64.1 %shard_map.59 = (f32[1024,256]{1,0:T(8,128)}, f32[256,256]{1,0:T(8,128)}, bf16[1024,1536]{1,0:T(8,128)(2,1)}) custom-call(bf16[1024,512]{1,0:T(8,128)(2,1)} %tex_ref.1, bf16[1536,512]{1,0:T(8,128)(2,1)} %feat_ref.1, bf16[1536,256]{1,0:T(8,128)(2,1)} %sketch_ref.1, f32[1024,1]{1,0:T(8,128)} %fusion.2.used_ref, f32[1,256]{1,0:T(1,128)} %broadcast_in_dim.4.count_ref), custom_call_target="tpu_custom_call" | custom-call | tf_op jit(solution)/shard_map/pallas_call | solution.py:227
  70.1 2.3 %fusion.3 = f32[1024,256]{1,0:T(8,128)S(1)} fusion(f32[1024,256]{1,0:T(8,128)} %get-tuple-element.5, f32[256,256]{1,0:T(8,128)} %get-tuple-element.6), kind=kOutput, calls=%fused_computation.5 | convolution fusion | flops 805306368 | bytes 2359296 | tf_op jit(solution)/shard_map/dot_general | solution.py:355
  72.4 0.0 copy-start
  72.5 4.4 %fusion.partial_ref = f32[256,1536]{1,0:T(8,128)} fusion(bf16[1024,1536]{1,0:T(8,128)(2,1)} %get-tuple-element.7, f32[1024,256]{1,0:T(8,128)S(1)} %fusion.3), kind=kOutput, calls=%fused_computation | convolution fusion | flops 805568512 | bytes 5767168 | tf_op jit(solution)/shard_map/dot_general | solution.py:357
  76.9 14.4 %shard_map.60 = f32[32,1536]{1,0:T(8,128)} custom-call(f32[256,1536]{1,0:T(8,128)} %fusion.partial_ref), custom_call_target="tpu_custom_call" | custom-call | tf_op jit(solution)/shard_map/pallas_call | solution.py:331
  91.2 0.0 copy-done
  91.2 1.6 %broadcast_divide_fusion = f32[32,1536]{1,0:T(8,128)} fusion(f32[32,1536]{1,0:T(8,128)} %shard_map.60, f32[]{:T(128)S(6)} %sqrt.3), kind=kLoop, calls=%fused_computation.4 | loop fusion | flops 49152 | bytes 393220 | tf_op jit(solution)/shard_map/div | solution.py:360
Async XLA Ops:
  72.4 18.8 %copy-start = (f32[1024,256]{1,0:T(8,128)}, f32[1024,256]{1,0:T(8,128)S(1)}, u32[]{:S(2)}) copy-start(f32[1024,256]{1,0:T(8,128)S(1)} %fusion.3) | copy-start | bytes 3145732
where the time goes:
time: 93.1 us; the launch traced here: 92.9 us
  Pallas kernels  78.5 us (84%)
  matrix products  6.69 us (7%)
  other arithmetic  4.45 us (5%)
  local copies, waits for them, and re-layouts  1.89 us (2%)
  between operations  1.37 us (1%)
    pallas_call x1, Pallas kernels, reduced(): pl.pallas_call(functools.partial(sketch_and_gram, n_texel, n_light), out_...  64.1 us
    pallas_call x1, Pallas kernels, scattered(): pl.pallas_call(functools.partial(scatter_sum, n_texel), out_shape=jax.Sha...  14.4 us
    dot_general x1, matrix products, on_device(): lax.dot_general(basis_half, tile_block, (((0,), (0,)), ((), ())), preferr...  4.4 us
    dot_general x1, matrix products, on_device(): lax.dot_general(sketched, inverse, (((1,), (1,)), ((), ())), precision=HI...  2.28 us

commit v1 on v0

--- a/solution.py
+++ b/solution.py
@@ -99,16 +99,22 @@
 
 
 def sketch_and_gram(
-    n_texel, n_light, tex_ref, feat_ref, sketch_ref, used_ref, count_ref, whole_ref, inverse_ref, tile_ref,
+    n_texel, n_light, tex_ref, feat_ref, sketch_ref, counts_ref, basis_ref, coeffs_ref,
+    tile_ref, inverse_ref, half_ref, product_ref, held, arrived,
     logits, partial_ref,
     landed, whole, pieces, plane, column, gram, scaled, work,
     part_send, part_recv, plane_send, plane_recv, column_send, column_recv,
-    full_send, full_recv, row_send, row_recv,
+    full_send, full_recv, row_send, row_recv, out_send, out_recv,
 ):
     texel, light = lax.axis_index("texel"), lax.axis_index("light")
     depth = partial_ref.shape[0] // n_light
     size = partial_ref.shape[1]
     piece = size // n_texel
+    own_count = counts_ref[texel]
+    valid = counts_ref[0]
+    for index in range(1, n_texel):
+        valid = valid + counts_ref[index]
+    valid = valid.astype(jnp.float32)
     lights = [lax.rem(light + d, n_light) for d in range(n_light)]
     texels = [lax.rem(texel + d, n_texel) for d in range(n_texel)]
     greet([(texel, lights[d]) for d in range(1, n_light)] + [(texels[d], light) for d in range(1, n_texel)])
@@ -144,9 +150,9 @@
 
         lax.fori_loop(0, feat_ref.shape[0] // step, block, 0)
         rows = rows_of(index, depth)
-        partial_ref[rows, :] = (
-            jnp.dot(tile_ref[rows, :], sketch_ref[...], preferred_element_type=jnp.float32) * used_ref[rows, :]
-        )
+        slot = index * depth + lax.broadcasted_iota(jnp.int32, (depth, size), 0)
+        product = jnp.dot(tile_ref[rows, :], sketch_ref[...], preferred_element_type=jnp.float32)
+        partial_ref[rows, :] = jnp.where(slot < own_count, product, 0.0)
 
     copies = []
     for d in range(1, n_light):
@@ -209,49 +215,21 @@
     ]
     for copy in copies:
         copy.wait()
-    scaled[...] = gram[...] / count_ref[...]
+    scaled[...] = gram[...] / valid
     factor_inverse(scaled, inverse_ref, work)
     for copy in gathers:
         copy.wait()
-    whole_ref[...] = whole[...]
-
-
-def reduced(tex_feat, light_feat, sketch, used, count, n_texel, n_light):
-    capacity, size = tex_feat.shape[0], sketch.shape[1]
-    lights = light_feat.shape[0]
-    step = next(w for w in (512, 256, 128) if lights % w == 0)
-    depth, piece = capacity // n_light, size // n_texel
-    vmem = pl.BlockSpec(memory_space=pltpu.VMEM)
-    f32 = jnp.float32
-    sems = pltpu.SemaphoreType.DMA
-    return pl.pallas_call(
-        functools.partial(sketch_and_gram, n_texel, n_light),
-        out_shape=(
-            jax.ShapeDtypeStruct((capacity, size), f32),
-            jax.ShapeDtypeStruct((size, size), f32),
-            jax.ShapeDtypeStruct((capacity, lights), jnp.bfloat16),
-        ),
-        in_specs=[vmem] * 5,
-        out_specs=(vmem, vmem, vmem),
-        scratch_shapes=[
-            pltpu.VMEM((depth, step), f32),
-            pltpu.VMEM((capacity, size), f32),
-            pltpu.VMEM((n_light, depth, size), f32),
-            pltpu.VMEM((capacity, size), f32),
-            pltpu.VMEM((n_texel, piece, size), f32),
-            pltpu.VMEM((n_texel, piece, size), f32),
-            pltpu.VMEM((n_light, piece, size), f32),
-            pltpu.VMEM((size, size), f32),
-            pltpu.VMEM((size, size), f32),
-            pltpu.VMEM((size, size), f32),
-            sems((n_light,)), sems((n_light,)),
-            sems((n_texel,)), sems((n_texel,)),
-            sems((n_light,)), sems((n_light,)),
-            sems((2, n_light)), sems((2, n_light)),
-            sems((n_texel,)), sems((n_texel,)),
-        ],
-        compiler_params=pltpu.CompilerParams(collective_id=1, has_side_effects=True),
-    )(tex_feat, light_feat, sketch, used, count)
+    for index in range(n_light):
+        rows = slice(index * depth, (index + 1) * depth)
+        basis = lax.dot_general(
+            whole[rows, :], inverse_ref[...], (((1,), (1,)), ((), ())), precision=HIGHEST,
+            preferred_element_type=jnp.float32,
+        )
+        basis_ref[rows, :] = basis
+        half_ref[rows, :] = basis.astype(jnp.bfloat16)
+    scatter_sum(
+        n_texel, half_ref, tile_ref, product_ref, coeffs_ref, valid, held, arrived, out_send, out_recv
+    )
 
 
 def halving_order(bits, last_first):
@@ -259,12 +237,11 @@
     return [0] + (rest[::-1] if last_first else rest)
 
 
-def scatter_sum(n_texel, partial_ref, out_ref, held, landed, send_sem, recv_sem):
+def scatter_sum(n_texel, half_ref, tile_ref, partial_ref, out_ref, valid, held, landed, send_sem, recv_sem):
     texel, light = lax.axis_index("texel"), lax.axis_index("light")
     bits = n_texel.bit_length() - 1
     bit = [lax.rem(texel // (1 << b), 2) for b in range(bits)]
     partner = [texel + (1 - 2 * bit[b]) * (1 << b) for b in range(bits)]
-    greet([(partner[b], light) for b in range(bits)])
     piece = partial_ref.shape[0] // n_texel
     width = partial_ref.shape[1] // 2
 
@@ -275,10 +252,19 @@
             block = block + flipped * (1 << b)
         return pl.multiple_of(block * piece, piece)
 
+    def multiply(half):
+        columns = slice(half * width, (half + 1) * width)
+        partial_ref[:, columns] = lax.dot_general(
+            half_ref[...], tile_ref[:, columns], (((0,), (0,)), ((), ())), preferred_element_type=jnp.float32
+        )
+
     orders = [halving_order(bits, False), halving_order(bits, True)]
+    root = jnp.sqrt(jnp.full((piece, width), valid))
     flights = [{}, {}]
     for step in range(bits):
         for half, order in enumerate(orders):
+            if step == 0:
+                multiply(half)
             b = order[step]
             left = [m for m in range(n_texel) if all(not m >> done & 1 for done in order[:step])]
             later = order[step + 1 :]
@@ -321,44 +307,53 @@
         columns = pl.ds(half * width, width)
         flights[half].pop((bits - 1, 0)).wait()
         below = partial_ref[pl.ds(start_of(0), piece), columns] if bits == 1 else held[half, 0]
-        out_ref[:, half * width : (half + 1) * width] = below + landed[half, bits - 1, 0]
-
-
-def scattered(partial, n_texel):
-    size, lights = partial.shape
-    piece, width, bits = size // n_texel, lights // 2, n_texel.bit_length() - 1
+        out_ref[:, half * width : (half + 1) * width] = (below + landed[half, bits - 1, 0]) / root
+
+
+def on_device(n_texel, n_light, tex_feat, light_feat, sketch, row_counts):
+    capacity, size = tex_feat.shape[0], sketch.shape[1]
+    lights = light_feat.shape[0]
+    step = next(w for w in (512, 256, 128) if lights % w == 0)
+    depth, piece = capacity // n_light, size // n_texel
+    width, bits = lights // 2, n_texel.bit_length() - 1
     vmem = pl.BlockSpec(memory_space=pltpu.VMEM)
+    smem = pl.BlockSpec(memory_space=pltpu.SMEM)
+    f32, half = jnp.float32, jnp.bfloat16
+    sems = pltpu.SemaphoreType.DMA
     return pl.pallas_call(
-        functools.partial(scatter_sum, n_texel),
-        out_shape=jax.ShapeDtypeStruct((piece, lights), jnp.float32),
-        in_specs=[vmem],
-        out_specs=vmem,
+        functools.partial(sketch_and_gram, n_texel, n_light),
+        out_shape=(
+            jax.ShapeDtypeStruct((capacity, size), f32),
+            jax.ShapeDtypeStruct((piece, lights), f32),
+        ),
+        in_specs=[vmem] * 3 + [smem],
+        out_specs=(vmem, vmem),
         scratch_shapes=[
-            pltpu.VMEM((2, n_texel, piece, width), jnp.float32),
-            pltpu.VMEM((2, bits, n_texel, piece, width), jnp.float32),
-            pltpu.SemaphoreType.DMA((2, bits, n_texel)),
-            pltpu.SemaphoreType.DMA((2, bits, n_texel)),
+            pltpu.VMEM((capacity, lights), half),
+            pltpu.VMEM((size, size), f32),
+            pltpu.VMEM((capacity, size), half),
+            pltpu.VMEM((size, lights), f32),
+            pltpu.VMEM((2, n_texel, piece, width), f32),
+            pltpu.VMEM((2, bits, n_texel, piece, width), f32),
+            pltpu.VMEM((depth, step), f32),
+            pltpu.VMEM((capacity, size), f32),
+            pltpu.VMEM((n_light, depth, size), f32),
+            pltpu.VMEM((capacity, size), f32),
+            pltpu.VMEM((n_texel, piece, size), f32),
+            pltpu.VMEM((n_texel, piece, size), f32),
+            pltpu.VMEM((n_light, piece, size), f32),
+            pltpu.VMEM((size, size), f32),
+            pltpu.VMEM((size, size), f32),
+            pltpu.VMEM((size, size), f32),
+            sems((n_light,)), sems((n_light,)),
+            sems((n_texel,)), sems((n_texel,)),
+            sems((n_light,)), sems((n_light,)),
+            sems((2, n_light)), sems((2, n_light)),
+            sems((n_texel,)), sems((n_texel,)),
+            sems((2, bits, n_texel)), sems((2, bits, n_texel)),
         ],
-        compiler_params=pltpu.CompilerParams(collective_id=2, has_side_effects=True),
-    )(partial)
-
-
-def on_device(n_texel, n_light, tex_feat, light_feat, sketch, row_counts):
-    capacity = tex_feat.shape[0]
-    own_count = row_counts[lax.axis_index("texel")]
-    valid_total = jnp.sum(row_counts).astype(jnp.float32)
-    row_valid = (lax.iota(jnp.int32, capacity) < own_count).astype(jnp.float32)
-    count = jnp.full((1, sketch.shape[1]), valid_total)
-    sketched, inverse, tile_block = reduced(
-        tex_feat, light_feat, sketch, row_valid[:, None], count, n_texel, n_light
-    )
-    basis = lax.dot_general(sketched, inverse, (((1,), (1,)), ((), ())), precision=HIGHEST)
-    basis_half = basis.astype(jnp.bfloat16)
-    partial_coeffs = lax.dot_general(
-        basis_half, tile_block, (((0,), (0,)), ((), ())), preferred_element_type=jnp.float32
-    )
-    coeffs = scattered(partial_coeffs, n_texel) / jnp.sqrt(valid_total)
-    return (basis, coeffs)
+        compiler_params=pltpu.CompilerParams(collective_id=1, has_side_effects=True),
+    )(tex_feat, light_feat, sketch, row_counts)
 
 
 def solution(mesh):

time: 93.1 us -> 80.2 us (0.86)
  matrix products: 6.69 us -> 0 us
  other arithmetic: 4.45 us -> 0 us
  Pallas kernels: 78.5 us -> 76.5 us
  local copies, waits for them, and re-layouts: 1.89 us -> 2.98 us
    dot_general x2 -> x0, matrix products: 6.69 us -> none  [the longest x1 4.4 us: on_device(): lax.dot_general(basis_half, tile_block, (((0,), (0,)), ((), ())), preferr...]
    unnamed x2 -> x4, local copies, waits for them, and re-layouts: 0.01 us -> 2.98 us
    pallas_call x2 -> x1, Pallas kernels: 78.5 us -> 76.5 us  [on_device(): pl.pallas_call(functools.partial(sketch_and_gram, n_texel, n_light), out_...]
    div x1 -> x0, other arithmetic: 1.63 us -> none  [on_device(): coeffs = scattered(partial_coeffs, n_texel) / jnp.sqrt(valid_total)]
    convert_element_type x1 -> x0, other arithmetic: 1.53 us -> none  [on_device(): row_valid = (lax.iota(jnp.int32, capacity) < own_count).astype(jnp.float32)]
    dynamic_slice x1 -> x0, local copies, waits for them, and re-layouts: 1.32 us -> none  [on_device(): own_count = row_counts[lax.axis_index('texel')]]
    reduce_sum x1 -> x0, other arithmetic: 1.29 us -> none  [on_device(): valid_total = jnp.sum(row_counts).astype(jnp.float32)]
where the time goes in v1:
time: 80.2 us; the launch traced here: 80.1 us
  Pallas kernels  76.5 us (95%)
  local copies, waits for them, and re-layouts  2.98 us (4%)
    pallas_call x1, Pallas kernels, on_device(): pl.pallas_call(functools.partial(sketch_and_gram, n_texel, n_light), out_...  76.5 us
    unnamed x4, local copies, waits for them, and re-layouts  2.98 us

profile of v1, /device:TPU:24, one launch (start us, length us, event | category | flops | bytes accessed | tf_op | source)
XLA Modules:
  0.0 80.1 jit_solution(6387245651009412426)
XLA Ops:
  0.6 76.5 %shard_map.59 = (f32[1024,256]{1,0:T(8,128)}, f32[32,1536]{1,0:T(8,128)}) custom-call(bf16[1024,512]{1,0:T(8,128)(2,1)} %tex_ref.1, bf16[1536,512]{1,0:T(8,128)(2,1)} %feat_ref.1, bf16[1536,256]{1,0:T(8,128)(2,1)} %sketch_ref.1, s32[8]{0:T(128)} %counts_ref.1), custom_call_target="tpu_custom_call" | custom-call | tf_op jit(solution)/shard_map/pallas_call | solution.py:323
  77.1 0.0 copy-start
  77.1 2.3 %copy.8 = f32[1024,256]{1,0:T(8,128)} copy(f32[1024,256]{1,0:T(8,128)} %get-tuple-element.4) | data formatting | bytes 2097152
  79.4 0.0 copy-done
  79.4 0.7 copy.9
Async XLA Ops:
  77.1 2.3 %copy-start = (f32[32,1536]{1,0:T(8,128)S(1)}, f32[32,1536]{1,0:T(8,128)}, u32[]{:S(2)}) copy-start(f32[32,1536]{1,0:T(8,128)} %get-tuple-element.5) | copy-start | bytes 589828

commit v2 on v1

--- a/solution.py
+++ b/solution.py
@@ -9,28 +9,19 @@
 
 HIGHEST = lax.Precision.HIGHEST
 BLOCK = 64
+CHUNK = 32
 INV_TWO_PI = 0.15915494309189535
-TWO_PI_HIGH = 6.28125
-TWO_PI_LOW = 0.001935307179586232
-SINE = (
-    0.9999999944783076,
-    -0.16666664569596037,
-    0.008333310280569169,
-    -0.00019840151040396647,
-    2.752937413742719e-06,
-    -2.4676261406891767e-08,
-    1.344908473337278e-10,
-)
+SINE = (6.283185273788226, -41.34167747777608, 81.60223120329199, -76.57499125549666, 39.71091094809089)
 
 
 def bounded_sine(x):
-    turns = jnp.round(x * INV_TWO_PI)
-    r = (x - turns * TWO_PI_HIGH) - turns * TWO_PI_LOW
-    s = r * r
-    value = jnp.full_like(s, SINE[-1])
-    for coefficient in SINE[-2::-1]:
+    turns = x * INV_TWO_PI - 0.25
+    z = 0.25 - jnp.abs(turns - jnp.round(turns))
+    s = z * z
+    value = SINE[-1] * s + SINE[-2]
+    for coefficient in SINE[-3::-1]:
         value = value * s + coefficient
-    return value * r
+    return value * z
 
 
 def eliminate(block):
@@ -91,24 +82,29 @@
 MESH_ID = pl.DeviceIdType.MESH
 
 
-def greet(peers):
-    barrier = pltpu.get_barrier_semaphore()
-    for peer in peers:
-        pl.semaphore_signal(barrier, inc=1, device_id=peer, device_id_type=MESH_ID)
-    pl.semaphore_wait(barrier, len(peers))
-
-
-def sketch_and_gram(
+def relay_order(chunks):
+    hop = 0.29 * chunks
+    events = [(c, "inward", c) for c in range(chunks)]
+    events += [(c + hop, "outward", c) for c in range(chunks)]
+    events += [(c + 3 * hop, "back_inward", c) for c in range(chunks)]
+    events += [(c + 4 * hop, "back_outward", c) for c in range(chunks)]
+    return [(kind, c) for _, kind, c in sorted(events)]
+
+
+def whole_step(
     n_texel, n_light, tex_ref, feat_ref, sketch_ref, counts_ref, basis_ref, coeffs_ref,
     tile_ref, inverse_ref, half_ref, product_ref, held, arrived,
-    logits, partial_ref,
+    logits_even, logits_odd, partial_ref,
     landed, whole, pieces, plane, column, gram, scaled, work,
-    part_send, part_recv, plane_send, plane_recv, column_send, column_recv,
-    full_send, full_recv, row_send, row_recv, out_send, out_recv,
+    sum_send, sum_recv, back_send, back_recv, plane_send, plane_recv, column_send, column_recv,
+    row_send, row_recv, out_send, out_recv,
 ):
     texel, light = lax.axis_index("texel"), lax.axis_index("light")
-    depth = partial_ref.shape[0] // n_light
-    size = partial_ref.shape[1]
+    capacity, size = partial_ref.shape
+    width = logits_even.shape[1]
+    block = logits_even.shape[0]
+    middle = capacity // 2
+    chunks = middle // CHUNK
     piece = size // n_texel
     own_count = counts_ref[texel]
     valid = counts_ref[0]
@@ -117,110 +113,162 @@
     valid = valid.astype(jnp.float32)
     lights = [lax.rem(light + d, n_light) for d in range(n_light)]
     texels = [lax.rem(texel + d, n_texel) for d in range(n_texel)]
-    greet([(texel, lights[d]) for d in range(1, n_light)] + [(texels[d], light) for d in range(1, n_texel)])
-
-    def send(source, target, send_sem, recv_sem, device):
-        copy = pltpu.make_async_remote_copy(
+    upper = light // (n_light // 2)
+    inward, outward = 1 - upper, upper
+    depth = light + upper * (n_light - 1 - 2 * light)
+    toward_middle = light + 1 - 2 * upper
+    toward_end = light - 1 + 2 * upper
+
+    barrier = pltpu.get_barrier_semaphore()
+    peers = [(texel, lights[d]) for d in range(1, n_light)] + [(texels[d], light) for d in range(1, n_texel)]
+    for peer in peers:
+        pl.semaphore_signal(barrier, inc=1, device_id=peer, device_id_type=MESH_ID)
+
+    def copy(source, target, send_sem, recv_sem, device):
+        return pltpu.make_async_remote_copy(
             src_ref=source, dst_ref=target, send_sem=send_sem, recv_sem=recv_sem,
             device_id=device, device_id_type=MESH_ID,
         )
-        copy.start()
-        return copy
 
     def rows_of(index, height):
         return pl.ds(pl.multiple_of(index * height, height), height)
 
-    step = logits.shape[1]
-
-    def fill(index):
-        texels_here = tex_ref[rows_of(index, depth), :]
-
-        def block(c, carry):
-            columns = rows_of(c, step)
-            logits[...] = lax.dot_general(
-                texels_here, feat_ref[columns, :], (((1,), (1,)), ((), ())), preferred_element_type=jnp.float32
+    def chunk_rows(half, c):
+        return pl.ds(pl.multiple_of(half * middle + c * CHUNK, CHUNK), CHUNK)
+
+    def sum_copy(half, c, to):
+        return copy(
+            partial_ref.at[chunk_rows(half, c)], landed.at[half, c],
+            sum_send.at[half, c], sum_recv.at[half, c], (texel, to),
+        )
+
+    def back_copy(half, c, to):
+        rows = chunk_rows(half, c)
+        return copy(
+            whole.at[rows], whole.at[rows], back_send.at[half, c], back_recv.at[half, c], (texel, to)
+        )
+
+    def fill(first):
+        rows = pl.ds(pl.multiple_of(first, block), block)
+        logits = (logits_even, logits_odd)
+        count = feat_ref.shape[0] // width
+
+        def product_of(c):
+            return lax.dot_general(
+                tex_ref[rows, :], feat_ref[c * width : (c + 1) * width, :], (((1,), (1,)), ((), ())),
+                preferred_element_type=jnp.float32,
             )
 
-            def strip(i, inner):
-                value = bounded_sine(logits[rows_of(i, 16), :]).astype(jnp.bfloat16)
-                tile_ref[pl.ds(pl.multiple_of(index * depth + i * 16, 16), 16), columns] = value
-                return inner
-
-            return lax.fori_loop(0, depth // 16, strip, carry, unroll=2)
-
-        lax.fori_loop(0, feat_ref.shape[0] // step, block, 0)
-        rows = rows_of(index, depth)
-        slot = index * depth + lax.broadcasted_iota(jnp.int32, (depth, size), 0)
+        logits[0][...] = product_of(0)
+        for c in range(count):
+            if c + 1 < count:
+                logits[(c + 1) % 2][...] = product_of(c + 1)
+            tile_ref[rows, c * width : (c + 1) * width] = bounded_sine(logits[c % 2][...]).astype(jnp.bfloat16)
+        slot = first + lax.broadcasted_iota(jnp.int32, (block, size), 0)
         product = jnp.dot(tile_ref[rows, :], sketch_ref[...], preferred_element_type=jnp.float32)
         partial_ref[rows, :] = jnp.where(slot < own_count, product, 0.0)
 
-    copies = []
-    for d in range(1, n_light):
-        fill(lights[d])
-        copies.append(
-            send(
-                partial_ref.at[rows_of(lights[d], depth)], landed.at[d],
-                part_send.at[d], part_recv.at[d], (texel, lights[d]),
-            )
-        )
-    fill(light)
-    own = partial_ref[rows_of(light, depth), :]
-    for d, copy in enumerate(copies, 1):
-        copy.wait()
-        own = own + landed[d]
-    whole[rows_of(light, depth), :] = own
-    early = depth // 4
-
-    def gather(part, first, height):
-        rows = pl.ds(pl.multiple_of(light * depth + first, 8), height)
-        return [
-            send(
-                whole.at[rows], whole.at[rows], full_send.at[part, d], full_recv.at[part, d], (texel, lights[d])
-            )
-            for d in range(1, n_light)
+    blocks = middle // block
+    per_block = block // CHUNK
+    for b in range(blocks):
+        fill(inward * middle + b * block)
+        if b == 0:
+            pl.semaphore_wait(barrier, len(peers))
+
+        @pl.when(depth == 0)
+        def _():
+            for c in range(b * per_block, (b + 1) * per_block):
+                sum_copy(inward, c, toward_middle).start()
+
+    for b in range(blocks):
+        fill(outward * middle + b * block)
+
+    @pl.when(depth == 0)
+    def _():
+        for c in range(chunks):
+            sum_copy(outward, c, toward_middle).wait_recv()
+            rows = chunk_rows(outward, c)
+            whole[rows, :] = partial_ref[rows, :] + landed[outward, c]
+            if c == 0:
+                for sent in range(chunks):
+                    sum_copy(inward, sent, toward_middle).wait_send()
+            back_copy(outward, c, toward_middle).start()
+        own = whole[pl.ds(pl.multiple_of(outward * middle, middle), middle), :]
+        local = lax.dot_general(
+            own, own, (((0,), (0,)), ((), ())), precision=HIGHEST, preferred_element_type=jnp.float32
+        )
+        for index in range(n_texel):
+            pieces[index] = local[index * piece : (index + 1) * piece, :]
+        copies = [
+            copy(pieces.at[texels[d]], plane.at[d], plane_send.at[d], plane_recv.at[d], (texels[d], light))
+            for d in range(1, n_texel)
         ]
-
-    gathers = gather(0, 0, early)
-    local = lax.dot_general(
-        own, own, (((0,), (0,)), ((), ())), precision=HIGHEST, preferred_element_type=jnp.float32
-    )
-    for index in range(n_texel):
-        pieces[index] = local[index * piece : (index + 1) * piece, :]
+        for going in copies:
+            going.start()
+        total = pieces[texel]
+        for d, going in enumerate(copies, 1):
+            going.wait()
+            total = total + plane[d]
+        column[upper] = total
+        for d in range(1, n_light):
+            copy(
+                column.at[upper], column.at[upper], column_send.at[d], column_recv.at[upper], (texel, lights[d])
+            ).start()
+
+    @pl.when(depth > 0)
+    def _():
+        for kind, c in relay_order(chunks):
+            if kind == "inward" or kind == "outward":
+                half, to = (inward, toward_middle) if kind == "inward" else (outward, toward_end)
+                going = sum_copy(half, c, to)
+                going.wait_recv()
+                rows = chunk_rows(half, c)
+                partial_ref[rows, :] = partial_ref[rows, :] + landed[half, c]
+                going.start()
+            else:
+                half, to = (outward, toward_middle) if kind == "back_inward" else (inward, toward_end)
+                going = back_copy(half, c, to)
+                going.wait_recv()
+                going.start()
+        copy(column.at[upper], column.at[upper], column_send.at[0], column_recv.at[upper], (texel, lights[1])).wait_recv()
+
+    other = 1 - upper
+    copy(column.at[other], column.at[other], column_send.at[0], column_recv.at[other], (texel, lights[1])).wait_recv()
+    gram[rows_of(texel, piece), :] = column[0] + column[1]
     copies = [
-        send(pieces.at[texels[d]], plane.at[d], plane_send.at[d], plane_recv.at[d], (texels[d], light))
+        copy(
+            gram.at[rows_of(texel, piece)], gram.at[rows_of(texel, piece)],
+            row_send.at[d], row_recv.at[d], (texels[d], light),
+        )
         for d in range(1, n_texel)
     ]
-    total = pieces[texel]
-    for d, copy in enumerate(copies, 1):
-        copy.wait()
-        total = total + plane[d]
-    column[light] = total
-    copies = [
-        send(column.at[light], column.at[light], column_send.at[d], column_recv.at[d], (texel, lights[d]))
-        for d in range(1, n_light)
-    ]
-    for copy in copies:
-        copy.wait()
-    gathers += gather(1, early, depth - early)
-    total = column[0]
-    for index in range(1, n_light):
-        total = total + column[index]
-    gram[rows_of(texel, piece), :] = total
-    copies = [
-        send(
-            gram.at[rows_of(texel, piece)], gram.at[rows_of(texel, piece)],
-            row_send.at[d], row_recv.at[d], (texels[d], light),
-        )
-        for d in range(1, n_texel)
-    ]
-    for copy in copies:
-        copy.wait()
+    for going in copies:
+        going.start()
+    for going in copies:
+        going.wait()
     scaled[...] = gram[...] / valid
     factor_inverse(scaled, inverse_ref, work)
-    for copy in gathers:
-        copy.wait()
-    for index in range(n_light):
-        rows = slice(index * depth, (index + 1) * depth)
+
+    @pl.when(depth == 0)
+    def _():
+        for c in range(chunks):
+            back_copy(inward, c, toward_middle).wait_recv()
+            back_copy(outward, c, toward_middle).wait_send()
+        for d in range(1, n_light):
+            copy(
+                column.at[upper], column.at[upper], column_send.at[d], column_recv.at[upper], (texel, lights[d])
+            ).wait_send()
+
+    @pl.when(depth > 0)
+    def _():
+        for c in range(chunks):
+            sum_copy(inward, c, toward_middle).wait_send()
+            sum_copy(outward, c, toward_end).wait_send()
+            back_copy(outward, c, toward_middle).wait_send()
+            back_copy(inward, c, toward_end).wait_send()
+
+    for index in range(capacity // block):
+        rows = slice(index * block, (index + 1) * block)
         basis = lax.dot_general(
             whole[rows, :], inverse_ref[...], (((1,), (1,)), ((), ())), precision=HIGHEST,
             preferred_element_type=jnp.float32,
@@ -310,22 +358,30 @@
         out_ref[:, half * width : (half + 1) * width] = (below + landed[half, bits - 1, 0]) / root
 
 
+def write_out(basis_ref, coeffs_ref, basis_out, coeffs_out, sems):
+    copies = [
+        pltpu.make_async_copy(basis_ref, basis_out, sems.at[0]),
+        pltpu.make_async_copy(coeffs_ref, coeffs_out, sems.at[1]),
+    ]
+    for going in copies:
+        going.start()
+    for going in copies:
+        going.wait()
+
+
 def on_device(n_texel, n_light, tex_feat, light_feat, sketch, row_counts):
     capacity, size = tex_feat.shape[0], sketch.shape[1]
     lights = light_feat.shape[0]
-    step = next(w for w in (512, 256, 128) if lights % w == 0)
-    depth, piece = capacity // n_light, size // n_texel
+    block, step = capacity // 4, next(w for w in (256, 128) if lights % w == 0)
+    chunks, piece = capacity // 2 // CHUNK, size // n_texel
     width, bits = lights // 2, n_texel.bit_length() - 1
     vmem = pl.BlockSpec(memory_space=pltpu.VMEM)
     smem = pl.BlockSpec(memory_space=pltpu.SMEM)
     f32, half = jnp.float32, jnp.bfloat16
     sems = pltpu.SemaphoreType.DMA
-    return pl.pallas_call(
-        functools.partial(sketch_and_gram, n_texel, n_light),
-        out_shape=(
-            jax.ShapeDtypeStruct((capacity, size), f32),
-            jax.ShapeDtypeStruct((piece, lights), f32),
-        ),
+    basis, coeffs = pl.pallas_call(
+        functools.partial(whole_step, n_texel, n_light),
+        out_shape=(pltpu.VMEM((capacity, size), f32), pltpu.VMEM((piece, lights), f32)),
         in_specs=[vmem] * 3 + [smem],
         out_specs=(vmem, vmem),
         scratch_shapes=[
@@ -335,25 +391,33 @@
             pltpu.VMEM((size, lights), f32),
             pltpu.VMEM((2, n_texel, piece, width), f32),
             pltpu.VMEM((2, bits, n_texel, piece, width), f32),
-            pltpu.VMEM((depth, step), f32),
+            pltpu.VMEM((block, step), f32),
+            pltpu.VMEM((block, step), f32),
             pltpu.VMEM((capacity, size), f32),
-            pltpu.VMEM((n_light, depth, size), f32),
+            pltpu.VMEM((2, chunks, CHUNK, size), f32),
             pltpu.VMEM((capacity, size), f32),
             pltpu.VMEM((n_texel, piece, size), f32),
             pltpu.VMEM((n_texel, piece, size), f32),
-            pltpu.VMEM((n_light, piece, size), f32),
+            pltpu.VMEM((2, piece, size), f32),
             pltpu.VMEM((size, size), f32),
             pltpu.VMEM((size, size), f32),
             pltpu.VMEM((size, size), f32),
-            sems((n_light,)), sems((n_light,)),
+            sems((2, chunks)), sems((2, chunks)),
+            sems((2, chunks)), sems((2, chunks)),
             sems((n_texel,)), sems((n_texel,)),
-            sems((n_light,)), sems((n_light,)),
-            sems((2, n_light)), sems((2, n_light)),
+            sems((n_light,)), sems((2,)),
             sems((n_texel,)), sems((n_texel,)),
             sems((2, bits, n_texel)), sems((2, bits, n_texel)),
         ],
         compiler_params=pltpu.CompilerParams(collective_id=1, has_side_effects=True),
     )(tex_feat, light_feat, sketch, row_counts)
+    return pl.pallas_call(
+        write_out,
+        out_shape=(jax.ShapeDtypeStruct((capacity, size), f32), jax.ShapeDtypeStruct((piece, lights), f32)),
+        in_specs=[vmem, vmem],
+        out_specs=(pl.BlockSpec(memory_space=pl.ANY),) * 2,
+        scratch_shapes=[sems((2,))],
+    )(*(pltpu.with_memory_space_constraint(x, pltpu.VMEM) for x in (basis, coeffs)))
 
 
 def solution(mesh):

time: 80.2 us -> 69.6 us (0.87)
  the two profiles are of different devices: /device:TPU:24 before, /device:TPU:0 now
where the time goes in v2:
time: 69.6 us; the launch traced here: 69.5 us
  Pallas kernels  68.7 us (99%)
  between operations  0.8 us (1%)
    pallas_call x1, Pallas kernels, on_device(): pl.pallas_call(functools.partial(whole_step, n_texel, n_light), out_shape...  67.6 us

profile of v2, /device:TPU:0, one launch (start us, length us, event | category | flops | bytes accessed | tf_op | source)
XLA Modules:
  0.0 69.5 jit_solution(5823824575738357629)
XLA Ops:
  0.6 67.6 %shard_map.59 = (f32[1024,256]{1,0:T(8,128)S(1)}, f32[32,1536]{1,0:T(8,128)S(1)}) custom-call(bf16[1024,512]{1,0:T(8,128)(2,1)} %tex_ref.1, bf16[1536,512]{1,0:T(8,128)(2,1)} %feat_ref.1, bf16[1536,256]{1,0:T(8,128)(2,1)} %sketch_ref.1, s32[8]{0:T(128)} %counts_ref.1), custom_call_target="tpu_custom_call" | custom-call | tf_op jit(solution)/shard_map/pallas_call | solution.py:382
  68.3 1.0 %shard_map.60 = (f32[1024,256]{1,0:T(8,128)}, f32[32,1536]{1,0:T(8,128)}) custom-call(f32[1024,256]{1,0:T(8,128)S(1)} %get-tuple-element.4.basis_ref, f32[32,1536]{1,0:T(8,128)S(1)} %get-tuple-element.5.coeffs_ref), custom_call_target="tpu_custom_call" | custom-call | tf_op jit(solution)/shard_map/pallas_call | solution.py:414

commit v3 on v2

--- a/solution.py
+++ b/solution.py
@@ -50,9 +50,8 @@
     return jnp.concatenate(rows, axis=0)
 
 
-def factor_inverse(gram_ref, inverse_ref, work_ref):
-    size = gram_ref.shape[0]
-    work_ref[...] = gram_ref[...]
+def factor_inverse(work_ref, inverse_ref, finish_gram):
+    size = work_ref.shape[0]
     row = lax.broadcasted_iota(jnp.int32, (size, size), 0)
     column = lax.broadcasted_iota(jnp.int32, (size, size), 1)
     inverse_ref[...] = jnp.where(row == column, 1.0, 0.0).astype(jnp.float32)
@@ -71,6 +70,8 @@
         left = jnp.dot(scaled, work_ref[own, :], precision=HIGHEST, preferred_element_type=jnp.float32)
         right = jnp.dot(scaled, inverse_ref[own, :], precision=HIGHEST, preferred_element_type=jnp.float32)
         inverse_ref[own, :] = right
+        if start == 0:
+            finish_gram()
         rest = size - start - BLOCK
         if rest:
             lower = slice(start + BLOCK, size)
@@ -82,10 +83,10 @@
 MESH_ID = pl.DeviceIdType.MESH
 
 
-def relay_order(chunks):
+def relay_order(chunks, relayed):
     hop = 0.29 * chunks
-    events = [(c, "inward", c) for c in range(chunks)]
-    events += [(c + hop, "outward", c) for c in range(chunks)]
+    events = [(c, "inward", c) for c in range(relayed)]
+    events += [(c + hop, "outward", c) for c in range(relayed)]
     events += [(c + 3 * hop, "back_inward", c) for c in range(chunks)]
     events += [(c + 4 * hop, "back_outward", c) for c in range(chunks)]
     return [(kind, c) for _, kind, c in sorted(events)]
@@ -95,9 +96,10 @@
     n_texel, n_light, tex_ref, feat_ref, sketch_ref, counts_ref, basis_ref, coeffs_ref,
     tile_ref, inverse_ref, half_ref, product_ref, held, arrived,
     logits_even, logits_odd, partial_ref,
-    landed, whole, pieces, plane, column, gram, scaled, work,
-    sum_send, sum_recv, back_send, back_recv, plane_send, plane_recv, column_send, column_recv,
-    row_send, row_recv, out_send, out_recv,
+    landed, straight, whole, work,
+    pieces_first, pieces_rest, plane_first, plane_rest, column_first, column_rest, rows_first, rows_rest,
+    sum_send, sum_recv, straight_send, straight_recv, back_send, back_recv,
+    plane_send, plane_recv, column_send, column_recv, row_send, row_recv, out_send, out_recv,
 ):
     texel, light = lax.axis_index("texel"), lax.axis_index("light")
     capacity, size = partial_ref.shape
@@ -105,7 +107,8 @@
     block = logits_even.shape[0]
     middle = capacity // 2
     chunks = middle // CHUNK
-    piece = size // n_texel
+    direct = straight.shape[2]
+    relayed = chunks - direct
     own_count = counts_ref[texel]
     valid = counts_ref[0]
     for index in range(1, n_texel):
@@ -116,6 +119,7 @@
     upper = light // (n_light // 2)
     inward, outward = 1 - upper, upper
     depth = light + upper * (n_light - 1 - 2 * light)
+    inner = 1 - (n_light // 2 - depth) // (n_light // 2)
     toward_middle = light + 1 - 2 * upper
     toward_end = light - 1 + 2 * upper
 
@@ -130,9 +134,6 @@
             device_id=device, device_id_type=MESH_ID,
         )
 
-    def rows_of(index, height):
-        return pl.ds(pl.multiple_of(index * height, height), height)
-
     def chunk_rows(half, c):
         return pl.ds(pl.multiple_of(half * middle + c * CHUNK, CHUNK), CHUNK)
 
@@ -141,6 +142,16 @@
             partial_ref.at[chunk_rows(half, c)], landed.at[half, c],
             sum_send.at[half, c], sum_recv.at[half, c], (texel, to),
         )
+
+    def straight_copy(half, place, c, to):
+        return copy(
+            partial_ref.at[chunk_rows(half, relayed + c)], straight.at[half, place, c],
+            straight_send.at[half, c], straight_recv.at[half, place, c], (texel, to),
+        )
+
+    def straight_own(half, c):
+        place = half * light + (1 - half) * (n_light - 1 - light)
+        return straight_copy(half, place, c, half * (n_light - 1))
 
     def back_copy(half, c, to):
         rows = chunk_rows(half, c)
@@ -170,54 +181,99 @@
 
     blocks = middle // block
     per_block = block // CHUNK
-    for b in range(blocks):
-        fill(inward * middle + b * block)
-        if b == 0:
+    for turn in range(2 * blocks):
+        edge_half, edge_block = turn // blocks, turn % blocks
+        inner_half, inner_block = turn % 2, blocks - 1 - turn // 2
+        is_outward = (1 - inner) * edge_half + inner * inner_half
+        which = (1 - inner) * edge_block + inner * inner_block
+        fill((inward * (1 - is_outward) + outward * is_outward) * middle + which * block)
+        if turn == 0:
             pl.semaphore_wait(barrier, len(peers))
 
-        @pl.when(depth == 0)
+        @pl.when(inner == 0)
         def _():
-            for c in range(b * per_block, (b + 1) * per_block):
-                sum_copy(inward, c, toward_middle).start()
-
-    for b in range(blocks):
-        fill(outward * middle + b * block)
-
-    @pl.when(depth == 0)
+            if edge_half == 0:
+                for c in range(edge_block * per_block, (edge_block + 1) * per_block):
+                    if c < relayed:
+                        sum_copy(inward, c, toward_middle).start()
+                    else:
+                        straight_own(inward, c - relayed).start()
+
+        @pl.when(inner == 1)
+        def _():
+            for c in range(inner_block * per_block, (inner_block + 1) * per_block):
+                if c >= relayed:
+                    straight_own(inward if inner_half == 0 else outward, c - relayed).start()
+
+    groups = (
+        (pieces_first, plane_first, column_first, rows_first),
+        (pieces_rest, plane_rest, column_rest, rows_rest),
+    )
+    quarter = size // 4
+
+    @pl.when(inner == 0)
     def _():
         for c in range(chunks):
-            sum_copy(outward, c, toward_middle).wait_recv()
             rows = chunk_rows(outward, c)
-            whole[rows, :] = partial_ref[rows, :] + landed[outward, c]
+            if c < relayed:
+                sum_copy(outward, c, toward_middle).wait_recv()
+                whole[rows, :] = partial_ref[rows, :] + landed[outward, c]
+            else:
+                total = partial_ref[rows, :]
+                for place in range(n_light - 1):
+                    straight_copy(outward, place, c - relayed, toward_middle).wait_recv()
+                    total = total + straight[outward, place, c - relayed]
+                whole[rows, :] = total
             if c == 0:
-                for sent in range(chunks):
+                for sent in range(relayed):
                     sum_copy(inward, sent, toward_middle).wait_send()
+                for sent in range(direct):
+                    straight_own(inward, sent).wait_send()
             back_copy(outward, c, toward_middle).start()
         own = whole[pl.ds(pl.multiple_of(outward * middle, middle), middle), :]
         local = lax.dot_general(
             own, own, (((0,), (0,)), ((), ())), precision=HIGHEST, preferred_element_type=jnp.float32
         )
+        rest = jnp.concatenate(
+            [local[2 * quarter : 3 * quarter, 2 * quarter :], local[3 * quarter :, 2 * quarter :]], axis=1
+        )
+        rest = jnp.concatenate([local[quarter : 2 * quarter, :], rest], axis=0)
         for index in range(n_texel):
-            pieces[index] = local[index * piece : (index + 1) * piece, :]
+            for part, ref in ((local, pieces_first), (rest, pieces_rest)):
+                height = ref.shape[1]
+                ref[index] = part[index * height : (index + 1) * height, :]
         copies = [
-            copy(pieces.at[texels[d]], plane.at[d], plane_send.at[d], plane_recv.at[d], (texels[d], light))
-            for d in range(1, n_texel)
+            [
+                copy(
+                    pieces.at[texels[d]], plane.at[d], plane_send.at[g, d], plane_recv.at[g, d], (texels[d], light)
+                )
+                for d in range(1, n_texel)
+            ]
+            for g, (pieces, plane, _, _) in enumerate(groups)
         ]
-        for going in copies:
+        for going in copies[0] + copies[1]:
             going.start()
-        total = pieces[texel]
-        for d, going in enumerate(copies, 1):
-            going.wait()
-            total = total + plane[d]
-        column[upper] = total
-        for d in range(1, n_light):
-            copy(
-                column.at[upper], column.at[upper], column_send.at[d], column_recv.at[upper], (texel, lights[d])
-            ).start()
-
-    @pl.when(depth > 0)
+        for g, (pieces, plane, column, _) in enumerate(groups):
+            total = pieces[texel]
+            for d, going in enumerate(copies[g], 1):
+                going.wait()
+                total = total + plane[d]
+            column[upper] = total
+            for d in range(1, n_light):
+                copy(
+                    column.at[upper], column.at[upper], column_send.at[g, d], column_recv.at[g, upper],
+                    (texel, lights[d]),
+                ).start()
+
+    def column_wait(g, side):
+        column = groups[g][2]
+        copy(
+            column.at[side], column.at[side], column_send.at[g, 0], column_recv.at[g, side], (texel, lights[1])
+        ).wait_recv()
+
+    @pl.when(inner == 1)
     def _():
-        for kind, c in relay_order(chunks):
+        for kind, c in relay_order(chunks, relayed):
             if kind == "inward" or kind == "outward":
                 half, to = (inward, toward_middle) if kind == "inward" else (outward, toward_end)
                 going = sum_copy(half, c, to)
@@ -230,53 +286,90 @@
                 going = back_copy(half, c, to)
                 going.wait_recv()
                 going.start()
-        copy(column.at[upper], column.at[upper], column_send.at[0], column_recv.at[upper], (texel, lights[1])).wait_recv()
-
-    other = 1 - upper
-    copy(column.at[other], column.at[other], column_send.at[0], column_recv.at[other], (texel, lights[1])).wait_recv()
-    gram[rows_of(texel, piece), :] = column[0] + column[1]
-    copies = [
-        copy(
-            gram.at[rows_of(texel, piece)], gram.at[rows_of(texel, piece)],
-            row_send.at[d], row_recv.at[d], (texels[d], light),
-        )
-        for d in range(1, n_texel)
-    ]
-    for going in copies:
-        going.start()
-    for going in copies:
-        going.wait()
-    scaled[...] = gram[...] / valid
-    factor_inverse(scaled, inverse_ref, work)
-
-    @pl.when(depth == 0)
+        for g in range(2):
+            column_wait(g, upper)
+
+    row_copies = []
+    for g, (_, _, column, rows) in enumerate(groups):
+        column_wait(g, 1 - upper)
+        rows[texel] = column[0] + column[1]
+        row_copies.append(
+            [
+                copy(rows.at[texel], rows.at[texel], row_send.at[g, d], row_recv.at[g, texel], (texels[d], light))
+                for d in range(1, n_texel)
+            ]
+        )
+        for going in row_copies[g]:
+            going.start()
+
+    def row_wait(g):
+        rows = groups[g][3]
+        for d in range(1, n_texel):
+            copy(
+                rows.at[texels[d]], rows.at[texels[d]], row_send.at[g, d], row_recv.at[g, texels[d]], (texels[d], light)
+            ).wait_recv()
+
+    row_wait(0)
+    height = rows_first.shape[1]
+    for index in range(n_texel):
+        work[index * height : (index + 1) * height, :] = rows_first[index] / valid
+
+    def finish_gram():
+        row_wait(1)
+        height = rows_rest.shape[1]
+        rest = jnp.concatenate([rows_rest[index] for index in range(n_texel)], axis=0) / valid
+        work[quarter : 2 * quarter, :] = rest[:quarter, :]
+        work[2 * quarter :, : 2 * quarter] = jnp.zeros((2 * quarter, 2 * quarter), jnp.float32)
+        work[2 * quarter : 3 * quarter, 2 * quarter :] = rest[quarter:, : 2 * quarter]
+        work[3 * quarter :, 2 * quarter :] = rest[quarter:, 2 * quarter :]
+
+    factor_inverse(work, inverse_ref, finish_gram)
+
+    @pl.when(inner == 0)
     def _():
         for c in range(chunks):
             back_copy(inward, c, toward_middle).wait_recv()
             back_copy(outward, c, toward_middle).wait_send()
-        for d in range(1, n_light):
-            copy(
-                column.at[upper], column.at[upper], column_send.at[d], column_recv.at[upper], (texel, lights[d])
-            ).wait_send()
-
-    @pl.when(depth > 0)
+        for g in range(2):
+            column = groups[g][2]
+            for d in range(1, n_light):
+                copy(
+                    column.at[upper], column.at[upper], column_send.at[g, d], column_recv.at[g, upper],
+                    (texel, lights[d]),
+                ).wait_send()
+
+    @pl.when(inner == 1)
     def _():
         for c in range(chunks):
-            sum_copy(inward, c, toward_middle).wait_send()
-            sum_copy(outward, c, toward_end).wait_send()
+            if c < relayed:
+                sum_copy(inward, c, toward_middle).wait_send()
+                sum_copy(outward, c, toward_end).wait_send()
+            else:
+                straight_own(inward, c - relayed).wait_send()
+                straight_own(outward, c - relayed).wait_send()
             back_copy(outward, c, toward_middle).wait_send()
             back_copy(inward, c, toward_end).wait_send()
 
+    for going in row_copies[0] + row_copies[1]:
+        going.wait_send()
+
     for index in range(capacity // block):
         rows = slice(index * block, (index + 1) * block)
-        basis = lax.dot_general(
-            whole[rows, :], inverse_ref[...], (((1,), (1,)), ((), ())), precision=HIGHEST,
+        half_ref[:, rows] = lax.dot_general(
+            inverse_ref[...], whole[rows, :], (((1,), (1,)), ((), ())), precision=HIGHEST,
             preferred_element_type=jnp.float32,
-        )
-        basis_ref[rows, :] = basis
-        half_ref[rows, :] = basis.astype(jnp.bfloat16)
+        ).astype(jnp.bfloat16)
+
+    def basis_rows():
+        for index in range(capacity // block):
+            rows = slice(index * block, (index + 1) * block)
+            basis_ref[rows, :] = lax.dot_general(
+                whole[rows, :], inverse_ref[...], (((1,), (1,)), ((), ())), precision=HIGHEST,
+                preferred_element_type=jnp.float32,
+            )
+
     scatter_sum(
-        n_texel, half_ref, tile_ref, product_ref, coeffs_ref, valid, held, arrived, out_send, out_recv
+        n_texel, half_ref, tile_ref, product_ref, coeffs_ref, valid, held, arrived, out_send, out_recv, basis_rows
     )
 
 
@@ -285,7 +378,7 @@
     return [0] + (rest[::-1] if last_first else rest)
 
 
-def scatter_sum(n_texel, half_ref, tile_ref, partial_ref, out_ref, valid, held, landed, send_sem, recv_sem):
+def scatter_sum(n_texel, half_ref, tile_ref, partial_ref, out_ref, valid, held, landed, send_sem, recv_sem, meanwhile):
     texel, light = lax.axis_index("texel"), lax.axis_index("light")
     bits = n_texel.bit_length() - 1
     bit = [lax.rem(texel // (1 << b), 2) for b in range(bits)]
@@ -303,7 +396,7 @@
     def multiply(half):
         columns = slice(half * width, (half + 1) * width)
         partial_ref[:, columns] = lax.dot_general(
-            half_ref[...], tile_ref[:, columns], (((0,), (0,)), ((), ())), preferred_element_type=jnp.float32
+            half_ref[...], tile_ref[:, columns], (((1,), (0,)), ((), ())), preferred_element_type=jnp.float32
         )
 
     orders = [halving_order(bits, False), halving_order(bits, True)]
@@ -341,6 +434,8 @@
                 )
                 copy.start()
                 flights[half][step, kept] = copy
+        if step == 0:
+            meanwhile()
         if step:
             for half, order in enumerate(orders):
                 for key in [k for k in flights[half] if k[0] == step - 1]:
@@ -374,6 +469,7 @@
     lights = light_feat.shape[0]
     block, step = capacity // 4, next(w for w in (256, 128) if lights % w == 0)
     chunks, piece = capacity // 2 // CHUNK, size // n_texel
+    first, rest, direct = size // 4 // n_texel, size // 2 // n_texel, chunks // n_light
     width, bits = lights // 2, n_texel.bit_length() - 1
     vmem = pl.BlockSpec(memory_space=pltpu.VMEM)
     smem = pl.BlockSpec(memory_space=pltpu.SMEM)
@@ -387,7 +483,7 @@
         scratch_shapes=[
             pltpu.VMEM((capacity, lights), half),
             pltpu.VMEM((size, size), f32),
-            pltpu.VMEM((capacity, size), half),
+            pltpu.VMEM((size, capacity), half),
             pltpu.VMEM((size, lights), f32),
             pltpu.VMEM((2, n_texel, piece, width), f32),
             pltpu.VMEM((2, bits, n_texel, piece, width), f32),
@@ -395,18 +491,19 @@
             pltpu.VMEM((block, step), f32),
             pltpu.VMEM((capacity, size), f32),
             pltpu.VMEM((2, chunks, CHUNK, size), f32),
+            pltpu.VMEM((2, n_light, direct, CHUNK, size), f32),
             pltpu.VMEM((capacity, size), f32),
-            pltpu.VMEM((n_texel, piece, size), f32),
-            pltpu.VMEM((n_texel, piece, size), f32),
-            pltpu.VMEM((2, piece, size), f32),
             pltpu.VMEM((size, size), f32),
-            pltpu.VMEM((size, size), f32),
-            pltpu.VMEM((size, size), f32),
+            pltpu.VMEM((n_texel, first, size), f32), pltpu.VMEM((n_texel, rest, size), f32),
+            pltpu.VMEM((n_texel, first, size), f32), pltpu.VMEM((n_texel, rest, size), f32),
+            pltpu.VMEM((2, first, size), f32), pltpu.VMEM((2, rest, size), f32),
+            pltpu.VMEM((n_texel, first, size), f32), pltpu.VMEM((n_texel, rest, size), f32),
             sems((2, chunks)), sems((2, chunks)),
+            sems((2, direct)), sems((2, n_light, direct)),
             sems((2, chunks)), sems((2, chunks)),
-            sems((n_texel,)), sems((n_texel,)),
-            sems((n_light,)), sems((2,)),
-            sems((n_texel,)), sems((n_texel,)),
+            sems((2, n_texel)), sems((2, n_texel)),
+            sems((2, n_light)), sems((2, 2)),
+            sems((2, n_texel)), sems((2, n_texel)),
             sems((2, bits, n_texel)), sems((2, bits, n_texel)),
         ],
         compiler_params=pltpu.CompilerParams(collective_id=1, has_side_effects=True),

time: 69.6 us -> 65.7 us (0.944)
  Pallas kernels: 68.7 us -> 64.7 us
    pallas_call x1, Pallas kernels: 67.6 us -> 63.7 us  [on_device(): pl.pallas_call(functools.partial(whole_step, n_texel, n_light), out_shape...]
where the time goes in v3:
time: 65.7 us; the launch traced here: 65.5 us
  Pallas kernels  64.7 us (98%)
  between operations  0.8 us (1%)
    pallas_call x1, Pallas kernels, on_device(): pl.pallas_call(functools.partial(whole_step, n_texel, n_light), out_shape...  63.7 us

profile of v3, /device:TPU:0, one launch (start us, length us, event | category | flops | bytes accessed | tf_op | source)
XLA Modules:
  0.0 65.5 jit_solution(15178612230623477177)
XLA Ops:
  0.6 63.7 %shard_map.59 = (f32[1024,256]{1,0:T(8,128)S(1)}, f32[32,1536]{1,0:T(8,128)S(1)}) custom-call(bf16[1024,512]{1,0:T(8,128)(2,1)} %tex_ref.1, bf16[1536,512]{1,0:T(8,128)(2,1)} %feat_ref.1, bf16[1536,256]{1,0:T(8,128)(2,1)} %sketch_ref.1, s32[8]{0:T(128)} %counts_ref.1), custom_call_target="tpu_custom_call" | custom-call | tf_op jit(solution)/shard_map/pallas_call | solution.py:478
  64.3 1.0 %shard_map.60 = (f32[1024,256]{1,0:T(8,128)}, f32[32,1536]{1,0:T(8,128)}) custom-call(f32[1024,256]{1,0:T(8,128)S(1)} %get-tuple-element.4.basis_ref, f32[32,1536]{1,0:T(8,128)S(1)} %get-tuple-element.5.coeffs_ref), custom_call_target="tpu_custom_call" | custom-call | tf_op jit(solution)/shard_map/pallas_call | solution.py:511

commit v4 on v3

v4 whole, which is shorter than its diff:
```python
import functools

import jax
import jax.numpy as jnp
from jax import lax
from jax.experimental import pallas as pl
from jax.experimental.pallas import tpu as pltpu
from jax.sharding import PartitionSpec as P

HIGHEST = lax.Precision.HIGHEST
BLOCK = 64
CHUNK = 16
INV_TWO_PI = 0.15915494309189535
SINE = (6.283185273788226, -41.34167747777608, 81.60223120329199, -76.57499125549666, 39.71091094809089)


def bounded_sine(x):
    turns = x * INV_TWO_PI - 0.25
    z = 0.25 - jnp.abs(turns - jnp.round(turns))
    s = z * z
    value = SINE[-1] * s + SINE[-2]
    for coefficient in SINE[-3::-1]:
        value = value * s + coefficient
    return value * z


def eliminate(block):
    rows = [block[8 * t : 8 * t + 8, :] for t in range(8)]
    below = lax.broadcasted_iota(jnp.int32, (8, 128), 0)

    def line_of(value, k):
        return jnp.broadcast_to(value[k : k + 1, :], (8, 128))

    def lane_of(value, k):
        return jnp.broadcast_to(value[:, k : k + 1], (8, 128))

    own = [lane_of(rows[0], k) for k in range(8)]
    for p in range(8):
        columns = {(t, k): lane_of(rows[t], 8 * p + k) for t in range(p + 1, 8) for k in range(8)}
        ahead = [lane_of(rows[p + 1], 8 * p + 8 + k) for k in range(8)] if p < 7 else None
        for k in range(8):
            inverse = 1.0 / line_of(own[k], k)
            factor = jnp.where(below > k, own[k] * inverse, 0.0)
            entries = {later: line_of(own[later], k) for later in range(k + 1, 8)}
            for later, entry in entries.items():
                own[later] = own[later] - factor * entry
            pivot_row = line_of(rows[p], k)
            rows[p] = rows[p] - factor * pivot_row
            for t in range(p + 1, 8):
                factor = columns[t, k] * inverse
                if t == p + 1:
                    for later in range(8):
                        ahead[later] = ahead[later] - factor * line_of(columns[t, k], later)
                for later, entry in entries.items():
                    columns[t, later] = columns[t, later] - factor * entry
                rows[t] = rows[t] - factor * pivot_row
        own = ahead
    return jnp.concatenate(rows, axis=0)


def factor_inverse(work_ref, finish_gram):
    size = work_ref.shape[0]
    row = lax.broadcasted_iota(jnp.int32, (size, size), 0)
    column = lax.broadcasted_iota(jnp.int32, (size, size), 1)
    work_ref[:, size:] = jnp.where(row == column, 1.0, 0.0).astype(jnp.float32)
    lane = lax.broadcasted_iota(jnp.int32, (BLOCK, 128), 1)
    line = lax.broadcasted_iota(jnp.int32, (BLOCK, 128), 0)
    for start in range(0, size, BLOCK):
        own = slice(start, start + BLOCK)
        first = start // 128 * 128
        last = size + (start + BLOCK + 127) // 128 * 128
        tile = work_ref[own, first : first + 128]
        if start % 128:
            tile = pltpu.roll(tile, 64, 1)
        unit = jnp.where(lane - BLOCK == line, 1.0, 0.0)
        done = eliminate(jnp.where(lane < BLOCK, tile, unit))
        pivots = jnp.sum(jnp.where(lane == line, done, 0.0), axis=1, keepdims=True)
        scaled = pltpu.roll(done * lax.rsqrt(pivots), 64, 1)[:, :BLOCK]
        both = jnp.dot(scaled, work_ref[own, first:last], precision=HIGHEST, preferred_element_type=jnp.float32)
        work_ref[own, size:last] = both[:, size - first :]
        if start == 0:
            finish_gram()
        flipped = both[:, : size - first].T
        for lower in ((start + BLOCK, start + 2 * BLOCK), (start + 2 * BLOCK, size)):
            if lower[0] < min(lower[1], size):
                work_ref[lower[0] : lower[1], first:last] -= jnp.dot(
                    flipped[lower[0] - first : lower[1] - first, :], both,
                    precision=HIGHEST, preferred_element_type=jnp.float32,
                )


def split(value):
    high = value.astype(jnp.bfloat16)
    return high, (value - high.astype(jnp.float32)).astype(jnp.bfloat16)


def product(left, right):
    def one(a, b):
        return lax.dot_general(a, b, (((1,), (1,)), ((), ())), preferred_element_type=jnp.float32)

    return one(left[0], right[0]) + (one(left[0], right[1]) + one(left[1], right[0]))


MESH_ID = pl.DeviceIdType.MESH


def relay_order(chunks):
    hop = 0.29 * chunks
    events = [(c, "inward", c) for c in range(chunks)]
    events += [(c + hop, "outward", c) for c in range(chunks)]
    events += [(c + max(3 * hop, chunks + 3), "back_inward", c) for c in range(chunks)]
    events += [(c + hop + chunks + 1, "back_outward", c) for c in range(chunks)]
    events += [(hop + 1.7 * chunks + 4 * g, "column", g) for g in range(2)]
    return [(kind, c) for _, kind, c in sorted(events)]


def whole_step(
    n_texel, n_light, tex_hbm, feat_hbm, sketch_hbm, counts_hbm, basis_hbm, coeffs_hbm,
    tex_ref, feat_ref, sketch_ref, counts_ref, basis_ref, coeffs_ref,
    tile_ref, half_ref, product_ref, held, arrived,
    logits_even, logits_odd, partial_ref,
    landed, whole, work, gram, high, low,
    pieces_first, pieces_rest, plane_first, plane_rest, column_first, column_rest, rows_first, rows_rest,
    sum_send, back_send, chunk_recv,
    plane_send, plane_recv, column_send, column_recv, row_send, row_recv, out_send, out_recv,
    local_sems, tex_sems,
):
    texel, light = lax.axis_index("texel"), lax.axis_index("light")
    capacity, size = partial_ref.shape
    width = logits_even.shape[1]
    block = logits_even.shape[0]
    middle = capacity // 2
    chunks = middle // CHUNK
    upper = light // (n_light // 2)
    inward, outward = 1 - upper, upper
    blocks = middle // block
    turns = [(inward, 0, block // 2), (inward, block // 2, block // 2)]
    turns += [(inward, b * block, block) for b in range(1, blocks)]
    turns += [(outward, b * block, block) for b in range(blocks)]

    def turn_rows(half, offset, height):
        return pl.ds(pl.multiple_of(half * middle + offset, height), height)

    tex_copies = [
        pltpu.make_async_copy(tex_hbm.at[turn_rows(*turn)], tex_ref.at[turn_rows(*turn)], tex_sems.at[index])
        for index, turn in enumerate(turns)
    ]
    feat_copies = [
        pltpu.make_async_copy(
            feat_hbm.at[pl.ds(c * width, width)], feat_ref.at[pl.ds(c * width, width)], local_sems.at[4]
        )
        for c in range(feat_ref.shape[0] // width)
    ]
    sketch_copy = pltpu.make_async_copy(sketch_hbm, sketch_ref, local_sems.at[2])
    counts_copy = pltpu.make_async_copy(counts_hbm, counts_ref, local_sems.at[3])
    for going in tex_copies[:1] + feat_copies + [counts_copy, sketch_copy]:
        going.start()
    lights = [lax.rem(light + d, n_light) for d in range(n_light)]
    texels = [lax.rem(texel + d, n_texel) for d in range(n_texel)]
    depth = light + upper * (n_light - 1 - 2 * light)
    inner = 1 - (n_light // 2 - depth) // (n_light // 2)
    toward_middle = light + 1 - 2 * upper
    toward_end = light - 1 + 2 * upper

    barrier = pltpu.get_barrier_semaphore()
    peers = [(texel, lights[d]) for d in range(1, n_light)] + [(texels[d], light) for d in range(1, n_texel)]
    for peer in peers:
        pl.semaphore_signal(barrier, inc=1, device_id=peer, device_id_type=MESH_ID)

    def copy(source, target, send_sem, recv_sem, device):
        return pltpu.make_async_remote_copy(
            src_ref=source, dst_ref=target, send_sem=send_sem, recv_sem=recv_sem,
            device_id=device, device_id_type=MESH_ID,
        )

    def chunk_rows(half, c):
        return pl.ds(pl.multiple_of(half * middle + c * CHUNK, CHUNK), CHUNK)

    def sum_copy(half, c, to):
        return copy(
            partial_ref.at[chunk_rows(half, c)], landed.at[half, c],
            sum_send.at[half], chunk_recv.at[half, c], (texel, to),
        )

    def all_sent(ref, sems, half):
        rows = ref.at[pl.ds(pl.multiple_of(half * middle, middle), middle)]
        copy(rows, rows, sems.at[half], chunk_recv.at[half, 0], (texel, toward_middle)).wait_send()

    def back_copy(half, c, to):
        rows = chunk_rows(half, c)
        return copy(
            whole.at[rows], whole.at[rows], back_send.at[half], chunk_recv.at[half, c], (texel, to)
        )

    def fill(turn):
        half, offset, height = turns[turn]
        rows = turn_rows(half, offset, height)
        logits = (logits_even.at[pl.ds(0, height)], logits_odd.at[pl.ds(0, height)])
        count = feat_ref.shape[0] // width

        def product_of(c):
            return lax.dot_general(
                tex_ref[rows, :], feat_ref[c * width : (c + 1) * width, :], (((1,), (1,)), ((), ())),
                preferred_element_type=jnp.float32,
            )

        tex_copies[turn].wait()
        if turn == 0:
            pltpu.make_async_copy(feat_hbm, feat_ref, local_sems.at[4]).wait()
            for going in tex_copies[1:]:
                going.start()
        logits[0][...] = product_of(0)
        for c in range(count):
            if c + 1 < count:
                logits[(c + 1) % 2][...] = product_of(c + 1)
            tile_ref[rows, c * width : (c + 1) * width] = bounded_sine(logits[c % 2][...]).astype(jnp.bfloat16)
        if turn == 0:
            sketch_copy.wait()
            counts_copy.wait()
        own_count = counts_ref[texel]
        slot = half * middle + offset + lax.broadcasted_iota(jnp.int32, (height, size), 0)
        sums = jnp.dot(tile_ref[rows, :], sketch_ref[...], preferred_element_type=jnp.float32)
        partial_ref[rows, :] = jnp.where(slot < own_count, sums, 0.0)

    for turn, (_, offset, height) in enumerate(turns):
        fill(turn)
        if turn == 0:
            pl.semaphore_wait(barrier, len(peers))

        @pl.when(inner == 0)
        def _():
            if turn <= blocks:
                for c in range(offset // CHUNK, (offset + height) // CHUNK):
                    sum_copy(inward, c, toward_middle).start()

    def split_half(half):
        for index in range(blocks):
            rows = turn_rows(half, index * block, block)
            high[rows, :], low[rows, :] = split(whole[rows, :])

    groups = (
        (pieces_first, plane_first, column_first, rows_first),
        (pieces_rest, plane_rest, column_rest, rows_rest),
    )
    quarter = size // 4

    def column_wait(g, side):
        column = groups[g][2]
        copy(
            column.at[side], column.at[side], column_send.at[g], column_recv.at[g, side], (texel, lights[1])
        ).wait_recv()

    def spread_rows(g):
        _, _, column, rows = groups[g]
        column_wait(g, 1 - upper)
        rows[texel] = column[0] + column[1]
        for d in range(1, n_texel):
            copy(rows.at[texel], rows.at[texel], row_send.at[g], row_recv.at[g], (texels[d], light)).start()

    @pl.when(inner == 0)
    def _():
        done = 0
        for c in range(chunks):
            rows = chunk_rows(outward, c)
            sum_copy(outward, c, toward_middle).wait_recv()
            whole[rows, :] = partial_ref[rows, :] + landed[outward, c]
            if c == 0:
                all_sent(partial_ref, sum_send, inward)
            back_copy(outward, c, toward_middle).start()
            if c + 1 in (chunks // 2, chunks * 3 // 4, chunks):
                height = (c + 1 - done) * CHUNK
                own = whole[pl.ds(pl.multiple_of(outward * middle + done * CHUNK, CHUNK), height), :]
                some = lax.dot_general(
                    own, own, (((0,), (0,)), ((), ())), precision=HIGHEST, preferred_element_type=jnp.float32
                )
                gram[...] = some if done == 0 else gram[...] + some
                done = c + 1
        local = gram[...]
        rest = jnp.concatenate(
            [local[2 * quarter : 3 * quarter, 2 * quarter :], local[3 * quarter :, 2 * quarter :]], axis=1
        )
        rest = jnp.concatenate([local[quarter : 2 * quarter, :], rest], axis=0)
        for index in range(n_texel):
            for part, ref in ((local, pieces_first), (rest, pieces_rest)):
                height = ref.shape[1]
                ref[index] = part[index * height : (index + 1) * height, :]
        copies = [
            [
                copy(
                    pieces.at[texels[d]], plane.at[d], plane_send.at[g], plane_recv.at[g], (texels[d], light)
                )
                for d in range(1, n_texel)
            ]
            for g, (pieces, plane, _, _) in enumerate(groups)
        ]
        for going in copies[0] + copies[1]:
            going.start()
        split_half(outward)
        for g, (pieces, plane, column, _) in enumerate(groups):
            total = pieces[texel]
            others = pl.ds(1, n_texel - 1)
            copy(pieces.at[others], plane.at[others], plane_send.at[g], plane_recv.at[g], (texels[1], light)).wait()
            for d in range(1, n_texel):
                total = total + plane[d]
            column[upper] = total
            for d in range(1, n_light):
                copy(
                    column.at[upper], column.at[upper], column_send.at[g], column_recv.at[g, upper],
                    (texel, lights[d]),
                ).start()
        for g in range(2):
            spread_rows(g)

    @pl.when(inner == 1)
    def _():
        for kind, c in relay_order(chunks):
            if kind == "column":
                column_wait(c, upper)
                spread_rows(c)
            elif kind == "inward" or kind == "outward":
                half, to = (inward, toward_middle) if kind == "inward" else (outward, toward_end)
                going = sum_copy(half, c, to)
                going.wait_recv()
                rows = chunk_rows(half, c)
                partial_ref[rows, :] = partial_ref[rows, :] + landed[half, c]
                going.start()
            else:
                half, to = (outward, toward_middle) if kind == "back_inward" else (inward, toward_end)
                going = back_copy(half, c, to)
                going.wait_recv()
                going.start()
        split_half(inward)
        split_half(outward)

    def row_whole(g):
        others = groups[g][3].at[pl.ds(1, n_texel - 1)]
        return copy(others, others, row_send.at[g], row_recv.at[g], (texels[1], light))

    valid = counts_ref[0]
    for index in range(1, n_texel):
        valid = valid + counts_ref[index]
    valid = valid.astype(jnp.float32)
    row_whole(0).wait_recv()
    height = rows_first.shape[1]
    for index in range(n_texel):
        work[index * height : (index + 1) * height, :size] = rows_first[index] / valid

    def finish_gram():
        @pl.when(inner == 0)
        def _():
            for c in range(chunks):
                back_copy(inward, c, toward_middle).wait_recv()

            split_half(inward)

        row_whole(1).wait_recv()
        height = rows_rest.shape[1]
        rest = jnp.concatenate([rows_rest[index] for index in range(n_texel)], axis=0) / valid
        work[quarter : 2 * quarter, :size] = rest[:quarter, :]
        work[2 * quarter :, : 2 * quarter] = jnp.zeros((2 * quarter, 2 * quarter), jnp.float32)
        work[2 * quarter : 3 * quarter, 2 * quarter : size] = rest[quarter:, : 2 * quarter]
        work[3 * quarter :, 2 * quarter : size] = rest[quarter:, 2 * quarter :]

    factor_inverse(work, finish_gram)
    inverse = split(work[:, size:])
    half_ref[...] = product(inverse, (high[...], low[...])).astype(jnp.bfloat16)
    basis_out = pltpu.make_async_copy(basis_ref, basis_hbm, local_sems.at[0])

    def basis_rows(step):
        rows = slice(step * middle, (step + 1) * middle)
        basis_ref[rows, :] = product((high[rows, :], low[rows, :]), inverse)
        if step == 1:
            basis_out.start()

    scatter_sum(
        n_texel, half_ref, tile_ref, product_ref, coeffs_ref, valid, held, arrived, out_send, out_recv, basis_rows
    )
    coeffs_out = pltpu.make_async_copy(coeffs_ref, coeffs_hbm, local_sems.at[1])
    coeffs_out.start()
    for half in range(2):
        sent = held.at[half, pl.ds(0, n_texel - 1)]
        copy(sent, sent, out_send.at[half], out_recv.at[half, 0], (texels[1], light)).wait_send()

    @pl.when(inner == 0)
    def _():
        all_sent(whole, back_send, outward)
        for g in range(2):
            sent = groups[g][1].at[pl.ds(0, n_light - 1)]
            copy(sent, sent, column_send.at[g], column_recv.at[g, upper], (texel, lights[1])).wait_send()

    @pl.when(inner == 1)
    def _():
        for half in (inward, outward):
            all_sent(partial_ref, sum_send, half)
            all_sent(whole, back_send, half)

    for g in range(2):
        row_whole(g).wait_send()
    basis_out.wait()
    coeffs_out.wait()


def halving_order(bits, last_first):
    rest = list(range(1, bits))
    return [0] + (rest[::-1] if last_first else rest)


def scatter_sum(n_texel, half_ref, tile_ref, partial_ref, out_ref, valid, held, landed, send_sem, recv_sem, meanwhile):
    texel, light = lax.axis_index("texel"), lax.axis_index("light")
    bits = n_texel.bit_length() - 1
    bit = [lax.rem(texel // (1 << b), 2) for b in range(bits)]
    partner = [texel + (1 - 2 * bit[b]) * (1 << b) for b in range(bits)]
    piece = partial_ref.shape[0] // n_texel
    width = partial_ref.shape[1] // 2

    def start_of(mask):
        block = 0
        for b in range(bits):
            flipped = 1 - bit[b] if mask >> b & 1 else bit[b]
            block = block + flipped * (1 << b)
        return pl.multiple_of(block * piece, piece)

    def multiply(half):
        columns = slice(half * width, (half + 1) * width)
        partial_ref[:, columns] = lax.dot_general(
            half_ref[...], tile_ref[:, columns], (((1,), (0,)), ((), ())), preferred_element_type=jnp.float32
        )

    orders = [halving_order(bits, False), halving_order(bits, True)]
    root = jnp.sqrt(jnp.full((piece, width), valid))
    flights = [{}, {}]
    used = [0, 0]
    for step in range(bits):
        for half, order in enumerate(orders):
            if step == 0:
                multiply(half)
            b = order[step]
            left = [m for m in range(n_texel) if all(not m >> done & 1 for done in order[:step])]
            later = order[step + 1 :]
            going = [m for m in left if m >> b & 1]
            going.sort(key=lambda m: [-(m >> c & 1) for c in later])
            columns = pl.ds(half * width, width)
            for m in going:
                kept = m - (1 << b)
                if step == 0:
                    source = partial_ref.at[pl.ds(start_of(m), piece), columns]
                else:
                    arrived = flights[half].pop((step - 1, m))
                    arrived.wait_recv()
                    below = (
                        partial_ref[pl.ds(start_of(m), piece), columns] if step == 1 else held[half, m]
                    )
                    held[half, m] = below + landed[half, step - 1, m]
                    source = held.at[half, m]
                copy = pltpu.make_async_remote_copy(
                    src_ref=source,
                    dst_ref=landed.at[half, step, kept],
                    send_sem=send_sem.at[half],
                    recv_sem=recv_sem.at[half, used[half]],
                    device_id=(partner[b], light),
                    device_id_type=MESH_ID,
                )
                copy.start()
                used[half] += 1
                flights[half][step, kept] = copy
        if step < 2:
            meanwhile(step)
        if step:
            for half, order in enumerate(orders):
                for key in [k for k in flights[half] if k[0] == step - 1]:
                    m = key[1]
                    flights[half].pop(key).wait_recv()
                    columns = pl.ds(half * width, width)
                    below = (
                        partial_ref[pl.ds(start_of(m), piece), columns] if step == 1 else held[half, m]
                    )
                    held[half, m] = below + landed[half, step - 1, m]
    for half in range(2):
        columns = pl.ds(half * width, width)
        flights[half].pop((bits - 1, 0)).wait_recv()
        below = partial_ref[pl.ds(start_of(0), piece), columns] if bits == 1 else held[half, 0]
        out_ref[:, half * width : (half + 1) * width] = (below + landed[half, bits - 1, 0]) / root


def write_out(basis_ref, coeffs_ref, basis_out, coeffs_out, sems):
    copies = [
        pltpu.make_async_copy(basis_ref, basis_out, sems.at[0]),
        pltpu.make_async_copy(coeffs_ref, coeffs_out, sems.at[1]),
    ]
    for going in copies:
        going.start()
    for going in copies:
        going.wait()


def on_device(n_texel, n_light, tex_feat, light_feat, sketch, row_counts):
    capacity, size = tex_feat.shape[0], sketch.shape[1]
    lights = light_feat.shape[0]
    block, step = capacity // 4, next(w for w in (256, 128) if lights % w == 0)
    chunks, piece = capacity // 2 // CHUNK, size // n_texel
    first, rest = size // 4 // n_texel, size // 2 // n_texel
    width, bits = lights // 2, n_texel.bit_length() - 1
    vmem = pl.BlockSpec(memory_space=pltpu.VMEM)
    anywhere = pl.BlockSpec(memory_space=pl.ANY)
    f32, half = jnp.float32, jnp.bfloat16
    sems = pltpu.SemaphoreType.DMA
    basis, coeffs = pl.pallas_call(
        functools.partial(whole_step, n_texel, n_light),
        out_shape=(pltpu.VMEM((capacity, size), f32), pltpu.VMEM((piece, lights), f32)),
        in_specs=[anywhere] * 4,
        out_specs=(anywhere, anywhere),
        scratch_shapes=[
            pltpu.VMEM(tex_feat.shape, half),
            pltpu.VMEM(light_feat.shape, half),
            pltpu.VMEM(sketch.shape, half),
            pltpu.SMEM(row_counts.shape, jnp.int32),
            pltpu.VMEM((capacity, size), f32),
            pltpu.VMEM((piece, lights), f32),
            pltpu.VMEM((capacity, lights), half),
            pltpu.VMEM((size, capacity), half),
            pltpu.VMEM((size, lights), f32),
            pltpu.VMEM((2, n_texel, piece, width), f32),
            pltpu.VMEM((2, bits, n_texel, piece, width), f32),
            pltpu.VMEM((block, step), f32),
            pltpu.VMEM((block, step), f32),
            pltpu.VMEM((capacity, size), f32),
            pltpu.VMEM((2, chunks, CHUNK, size), f32),
            pltpu.VMEM((capacity, size), f32),
            pltpu.VMEM((size, 2 * size), f32),
            pltpu.VMEM((size, size), f32),
            pltpu.VMEM((capacity, size), half),
            pltpu.VMEM((capacity, size), half),
            pltpu.VMEM((n_texel, first, size), f32), pltpu.VMEM((n_texel, rest, size), f32),
            pltpu.VMEM((n_texel, first, size), f32), pltpu.VMEM((n_texel, rest, size), f32),
            pltpu.VMEM((2, first, size), f32), pltpu.VMEM((2, rest, size), f32),
            pltpu.VMEM((n_texel, first, size), f32), pltpu.VMEM((n_texel, rest, size), f32),
            sems((2,)), sems((2,)), sems((2, chunks)),
            sems((2,)), sems((2,)),
            sems((2,)), sems((2, 2)),
            sems((2,)), sems((2,)),
            sems((2,)), sems((2, n_texel - 1)),
            sems((5,)), sems((5,)),
        ],
        compiler_params=pltpu.CompilerParams(collective_id=1, has_side_effects=True),
    )(tex_feat, light_feat, sketch, row_counts)
    return pl.pallas_call(
        write_out,
        out_shape=(jax.ShapeDtypeStruct((capacity, size), f32), jax.ShapeDtypeStruct((piece, lights), f32)),
        in_specs=[vmem, vmem],
        out_specs=(pl.BlockSpec(memory_space=pl.ANY),) * 2,
        scratch_shapes=[sems((2,))],
    )(*(pltpu.with_memory_space_constraint(x, pltpu.VMEM) for x in (basis, coeffs)))


def solution(mesh):
    placed = (P("texel", None), P("light", None), P("light", None), P())
    return jax.shard_map(
        functools.partial(on_device, mesh.shape["texel"], mesh.shape["light"]),
        mesh=mesh,
        in_specs=placed,
        out_specs=(P("texel", None), P("texel", "light")),
        check_vma=False,
    )
```

time: 65.7 us -> 61 us (0.928)
  Pallas kernels: 64.7 us -> 60.1 us
    pallas_call x1, Pallas kernels: 63.7 us -> 59 us  [on_device(): pl.pallas_call(functools.partial(whole_step, n_texel, n_light), out_shape...]
where the time goes in v4:
time: 61 us; the launch traced here: 60.9 us
  Pallas kernels  60.1 us (99%)
  between operations  0.8 us (1%)
    pallas_call x1, Pallas kernels, on_device(): pl.pallas_call(functools.partial(whole_step, n_texel, n_light), out_shape...  59 us

profile of v4, /device:TPU:0, one launch (start us, length us, event | category | flops | bytes accessed | tf_op | source)
XLA Modules:
  0.0 60.9 jit_solution(3544862279877858176)
XLA Ops:
  0.6 59.0 %shard_map.59 = (f32[1024,256]{1,0:T(8,128)S(1)}, f32[32,1536]{1,0:T(8,128)S(1)}) custom-call(bf16[1024,512]{1,0:T(8,128)(2,1)} %tex_hbm.1, bf16[1536,512]{1,0:T(8,128)(2,1)} %feat_hbm.1, bf16[1536,256]{1,0:T(8,128)(2,1)} %sketch_hbm.1, s32[8]{0:T(128)} %counts_hbm.1), custom_call_target="tpu_custom_call" | custom-call | tf_op jit(solution)/shard_map/pallas_call | solution.py:507
  59.7 1.0 %shard_map.60 = (f32[1024,256]{1,0:T(8,128)}, f32[32,1536]{1,0:T(8,128)}) custom-call(f32[1024,256]{1,0:T(8,128)S(1)} %get-tuple-element.4.basis_ref, f32[32,1536]{1,0:T(8,128)S(1)} %get-tuple-element.5.coeffs_ref), custom_call_target="tpu_custom_call" | custom-call | tf_op jit(solution)/shard_map/pallas_call | solution.py:546

commit v5 on v4

--- a/solution.py
+++ b/solution.py
@@ -58,7 +58,7 @@
     return jnp.concatenate(rows, axis=0)
 
 
-def factor_inverse(work_ref, finish_gram):
+def factor_inverse(work_ref, finish_gram, finish_rows):
     size = work_ref.shape[0]
     row = lax.broadcasted_iota(jnp.int32, (size, size), 0)
     column = lax.broadcasted_iota(jnp.int32, (size, size), 1)
@@ -80,6 +80,8 @@
         work_ref[own, size:last] = both[:, size - first :]
         if start == 0:
             finish_gram()
+        if start == 2 * BLOCK:
+            finish_rows()
         flipped = both[:, : size - first].T
         for lower in ((start + BLOCK, start + 2 * BLOCK), (start + 2 * BLOCK, size)):
             if lower[0] < min(lower[1], size):
@@ -104,14 +106,30 @@
 MESH_ID = pl.DeviceIdType.MESH
 
 
-def relay_order(chunks):
-    hop = 0.29 * chunks
-    events = [(c, "inward", c) for c in range(chunks)]
-    events += [(c + hop, "outward", c) for c in range(chunks)]
-    events += [(c + max(3 * hop, chunks + 3), "back_inward", c) for c in range(chunks)]
-    events += [(c + hop + chunks + 1, "back_outward", c) for c in range(chunks)]
-    events += [(hop + 1.7 * chunks + 4 * g, "column", g) for g in range(2)]
-    return [(kind, c) for _, kind, c in sorted(events)]
+def layout_of(capacity, n_light):
+    count = capacity // CHUNK
+    if n_light == 4:
+        shares = [count * 3 // 8, count // 8, count // 8, count * 3 // 8]
+    else:
+        shares = [count // 2] + [0] * (n_light - 2) + [count // 2]
+    return shares, [sum(shares[:z]) for z in range(n_light)]
+
+
+def relay_order(shares):
+    far, ends, owned = len(shares) - 1, shares[0], shares[1]
+    outgoing = [(far, c) for c in range(ends)] + [(2, c) for c in range(owned)]
+    hop = 8.3 if owned else 0.29 * ends
+    last = ends + owned + 2 * hop
+    events = [(i + hop, "inward", o, c) for i, (o, c) in enumerate(outgoing)]
+    events += [(c + 2 * hop, "outward", 0, c) for c in range(ends)]
+    if owned:
+        events += [(ends + c + 2 * hop, "final", 1, c) for c in range(owned)]
+        events += [(ends + c + 3 * hop, "back_outward", 2, c) for c in range(owned)]
+        events += [(last + 0.5, "plane", 0, 0), (last + 12.5, "column", 0, 0)]
+    events += [(last + 2 + c, "back_inward", 0, c) for c in range(ends)]
+    events += [(last + 2 + hop + c, "back_outward", far, c) for c in range(ends)]
+    events += [(last + 22 + 3 * g, "rows", 0, g) for g in range(2)]
+    return [event[1:] for event in sorted(events)]
 
 
 def whole_step(
@@ -119,9 +137,9 @@
     tex_ref, feat_ref, sketch_ref, counts_ref, basis_ref, coeffs_ref,
     tile_ref, half_ref, product_ref, held, arrived,
     logits_even, logits_odd, partial_ref,
-    landed, whole, work, gram, high, low,
+    landed, near, whole, work, gram, high, low,
     pieces_first, pieces_rest, plane_first, plane_rest, column_first, column_rest, rows_first, rows_rest,
-    sum_send, back_send, chunk_recv,
+    sum_send, back_send, chunk_recv, near_recv,
     plane_send, plane_recv, column_send, column_recv, row_send, row_recv, out_send, out_recv,
     local_sems, tex_sems,
 ):
@@ -130,20 +148,33 @@
     width = logits_even.shape[1]
     block = logits_even.shape[0]
     middle = capacity // 2
-    chunks = middle // CHUNK
+    shares, starts = layout_of(capacity, n_light)
+    far, ends, owned = n_light - 1, shares[0], shares[1]
+    owners = column_first.shape[0]
     upper = light // (n_light // 2)
-    inward, outward = 1 - upper, upper
-    blocks = middle // block
-    turns = [(inward, 0, block // 2), (inward, block // 2, block // 2)]
-    turns += [(inward, b * block, block) for b in range(1, blocks)]
-    turns += [(outward, b * block, block) for b in range(blocks)]
-
-    def turn_rows(half, offset, height):
-        return pl.ds(pl.multiple_of(half * middle + offset, height), height)
+
+    def chunk_of(o, c):
+        return starts[o] + c + upper * (starts[far - o] - starts[o])
+
+    def rows_at(o, c, height):
+        return pl.ds(pl.multiple_of(chunk_of(o, c) * CHUNK, CHUNK), height)
+
+    half_block = block // 2
+    per_half = half_block // CHUNK
+    turns = [(rows_at(far, 0, half_block), half_block, [(far, c) for c in range(per_half)])]
+    if owned:
+        turns += [(rows_at(far, per_half, block), block, [(far, c) for c in range(per_half, ends)])]
+        shared = pl.ds(starts[1] * CHUNK, block)
+        turns += [(shared, block, [(o, c) for o in (2, 1) for c in range(owned)])]
+        turns += [(rows_at(0, 0, block), block, []), (rows_at(0, 2 * per_half, half_block), half_block, [])]
+    else:
+        turns += [(rows_at(far, per_half, half_block), half_block, [(far, per_half + c) for c in range(per_half)])]
+        turns += [(rows_at(far, 2 * per_half, block), block, [(far, c) for c in range(2 * per_half, ends)])]
+        turns += [(rows_at(0, 0, block), block, []), (rows_at(0, 2 * per_half, block), block, [])]
 
     tex_copies = [
-        pltpu.make_async_copy(tex_hbm.at[turn_rows(*turn)], tex_ref.at[turn_rows(*turn)], tex_sems.at[index])
-        for index, turn in enumerate(turns)
+        pltpu.make_async_copy(tex_hbm.at[rows], tex_ref.at[rows], tex_sems.at[index])
+        for index, (rows, _, _) in enumerate(turns)
     ]
     feat_copies = [
         pltpu.make_async_copy(
@@ -159,8 +190,7 @@
     texels = [lax.rem(texel + d, n_texel) for d in range(n_texel)]
     depth = light + upper * (n_light - 1 - 2 * light)
     inner = 1 - (n_light // 2 - depth) // (n_light // 2)
-    toward_middle = light + 1 - 2 * upper
-    toward_end = light - 1 + 2 * upper
+    inward, outward = light + 1 - 2 * upper, light - 1 + 2 * upper
 
     barrier = pltpu.get_barrier_semaphore()
     peers = [(texel, lights[d]) for d in range(1, n_light)] + [(texels[d], light) for d in range(1, n_texel)]
@@ -173,28 +203,28 @@
             device_id=device, device_id_type=MESH_ID,
         )
 
-    def chunk_rows(half, c):
-        return pl.ds(pl.multiple_of(half * middle + c * CHUNK, CHUNK), CHUNK)
-
-    def sum_copy(half, c, to):
+    def sum_copy(o, c, to):
+        chunk = chunk_of(o, c)
         return copy(
-            partial_ref.at[chunk_rows(half, c)], landed.at[half, c],
-            sum_send.at[half], chunk_recv.at[half, c], (texel, to),
+            partial_ref.at[rows_at(o, c, CHUNK)], landed.at[chunk], sum_send, chunk_recv.at[chunk], (texel, to)
         )
 
-    def all_sent(ref, sems, half):
-        rows = ref.at[pl.ds(pl.multiple_of(half * middle, middle), middle)]
-        copy(rows, rows, sems.at[half], chunk_recv.at[half, 0], (texel, toward_middle)).wait_send()
-
-    def back_copy(half, c, to):
-        rows = chunk_rows(half, c)
-        return copy(
-            whole.at[rows], whole.at[rows], back_send.at[half], chunk_recv.at[half, c], (texel, to)
-        )
+    def near_copy(c, to):
+        return copy(partial_ref.at[rows_at(1, c, CHUNK)], near.at[c], sum_send, near_recv.at[c], (texel, to))
+
+    def back_copy(o, c, to):
+        rows = rows_at(o, c, CHUNK)
+        return copy(whole.at[rows], whole.at[rows], back_send, chunk_recv.at[chunk_of(o, c)], (texel, to))
+
+    def all_sent(sem, chunks):
+        while chunks:
+            some = min(chunks, capacity // CHUNK)
+            sent = whole.at[pl.ds(0, some * CHUNK)]
+            copy(sent, sent, sem, chunk_recv.at[0], (texel, inward)).wait_send()
+            chunks -= some
 
     def fill(turn):
-        half, offset, height = turns[turn]
-        rows = turn_rows(half, offset, height)
+        rows, height, _ = turns[turn]
         logits = (logits_even.at[pl.ds(0, height)], logits_odd.at[pl.ds(0, height)])
         count = feat_ref.shape[0] // width
 
@@ -218,24 +248,23 @@
             sketch_copy.wait()
             counts_copy.wait()
         own_count = counts_ref[texel]
-        slot = half * middle + offset + lax.broadcasted_iota(jnp.int32, (height, size), 0)
+        slot = rows.start + lax.broadcasted_iota(jnp.int32, (height, size), 0)
         sums = jnp.dot(tile_ref[rows, :], sketch_ref[...], preferred_element_type=jnp.float32)
         partial_ref[rows, :] = jnp.where(slot < own_count, sums, 0.0)
 
-    for turn, (_, offset, height) in enumerate(turns):
+    for turn, (_, _, ready) in enumerate(turns):
         fill(turn)
         if turn == 0:
             pl.semaphore_wait(barrier, len(peers))
 
         @pl.when(inner == 0)
         def _():
-            if turn <= blocks:
-                for c in range(offset // CHUNK, (offset + height) // CHUNK):
-                    sum_copy(inward, c, toward_middle).start()
-
-    def split_half(half):
-        for index in range(blocks):
-            rows = turn_rows(half, index * block, block)
+            for o, c in ready:
+                (near_copy(c, inward) if o == 1 and owned else sum_copy(o, c, inward)).start()
+
+    def split_rows(o):
+        if shares[o]:
+            rows = rows_at(o, 0, shares[o] * CHUNK)
             high[rows, :], low[rows, :] = split(whole[rows, :])
 
     groups = (
@@ -243,94 +272,112 @@
         (pieces_rest, plane_rest, column_rest, rows_rest),
     )
     quarter = size // 4
-
-    def column_wait(g, side):
-        column = groups[g][2]
-        copy(
-            column.at[side], column.at[side], column_send.at[g], column_recv.at[g, side], (texel, lights[1])
-        ).wait_recv()
-
-    def spread_rows(g):
-        _, _, column, rows = groups[g]
-        column_wait(g, 1 - upper)
-        rows[texel] = column[0] + column[1]
-        for d in range(1, n_texel):
-            copy(rows.at[texel], rows.at[texel], row_send.at[g], row_recv.at[g], (texels[d], light)).start()
-
-    @pl.when(inner == 0)
-    def _():
-        done = 0
-        for c in range(chunks):
-            rows = chunk_rows(outward, c)
-            sum_copy(outward, c, toward_middle).wait_recv()
-            whole[rows, :] = partial_ref[rows, :] + landed[outward, c]
-            if c == 0:
-                all_sent(partial_ref, sum_send, inward)
-            back_copy(outward, c, toward_middle).start()
-            if c + 1 in (chunks // 2, chunks * 3 // 4, chunks):
-                height = (c + 1 - done) * CHUNK
-                own = whole[pl.ds(pl.multiple_of(outward * middle + done * CHUNK, CHUNK), height), :]
-                some = lax.dot_general(
-                    own, own, (((0,), (0,)), ((), ())), precision=HIGHEST, preferred_element_type=jnp.float32
-                )
-                gram[...] = some if done == 0 else gram[...] + some
-                done = c + 1
+    own_column = light if owned else upper
+
+    def add_gram(o, first, chunks):
+        own = whole[rows_at(o, first, chunks * CHUNK), :]
+        some = lax.dot_general(
+            own, own, (((0,), (0,)), ((), ())), precision=HIGHEST, preferred_element_type=jnp.float32
+        )
+        gram[...] = gram[...] + some if first else some
+
+    def plane_start():
         local = gram[...]
         rest = jnp.concatenate(
             [local[2 * quarter : 3 * quarter, 2 * quarter :], local[3 * quarter :, 2 * quarter :]], axis=1
         )
         rest = jnp.concatenate([local[quarter : 2 * quarter, :], rest], axis=0)
-        for index in range(n_texel):
-            for part, ref in ((local, pieces_first), (rest, pieces_rest)):
-                height = ref.shape[1]
-                ref[index] = part[index * height : (index + 1) * height, :]
-        copies = [
-            [
+        for g, part in enumerate((local, rest)):
+            pieces, plane, _, _ = groups[g]
+            height = pieces.shape[1]
+            for index in range(n_texel):
+                pieces[index] = part[index * height : (index + 1) * height, :]
+            for d in range(1, n_texel):
                 copy(
                     pieces.at[texels[d]], plane.at[d], plane_send.at[g], plane_recv.at[g], (texels[d], light)
-                )
-                for d in range(1, n_texel)
-            ]
-            for g, (pieces, plane, _, _) in enumerate(groups)
-        ]
-        for going in copies[0] + copies[1]:
-            going.start()
-        split_half(outward)
+                ).start()
+
+    def column_start():
         for g, (pieces, plane, column, _) in enumerate(groups):
-            total = pieces[texel]
             others = pl.ds(1, n_texel - 1)
             copy(pieces.at[others], plane.at[others], plane_send.at[g], plane_recv.at[g], (texels[1], light)).wait()
+            total = pieces[texel]
             for d in range(1, n_texel):
                 total = total + plane[d]
-            column[upper] = total
+            column[own_column] = total
             for d in range(1, n_light):
                 copy(
-                    column.at[upper], column.at[upper], column_send.at[g], column_recv.at[g, upper],
+                    column.at[own_column], column.at[own_column], column_send.at[g], column_recv.at[g],
                     (texel, lights[d]),
                 ).start()
+
+    def rows_start(g, coming):
+        _, _, column, rows = groups[g]
+        some = column.at[pl.ds(0, coming)]
+        copy(some, some, column_send.at[g], column_recv.at[g], (texel, lights[1])).wait_recv()
+        total = column[0]
+        for index in range(1, owners):
+            total = total + column[index]
+        rows[texel] = total
+        for d in range(1, n_texel):
+            copy(rows.at[texel], rows.at[texel], row_send.at[g], row_recv.at[g], (texels[d], light)).start()
+
+    def column_sent():
         for g in range(2):
-            spread_rows(g)
+            sent = groups[g][1].at[pl.ds(0, n_light - 1)]
+            copy(sent, sent, column_send.at[g], column_recv.at[g], (texel, lights[1])).wait_send()
+
+    @pl.when(inner == 0)
+    def _():
+        done, held_back = 0, ends * 5 // 8
+        for c in range(ends):
+            rows = rows_at(0, c, CHUNK)
+            sum_copy(0, c, inward).wait_recv()
+            whole[rows, :] = partial_ref[rows, :] + landed[chunk_of(0, c)]
+            if c == held_back:
+                all_sent(sum_send, capacity // CHUNK - ends)
+                for earlier in range(c):
+                    back_copy(0, earlier, inward).start()
+            if c >= held_back:
+                back_copy(0, c, inward).start()
+            if c + 1 in (ends // 2, ends * 5 // 6, ends):
+                add_gram(0, done, c + 1 - done)
+                done = c + 1
+        plane_start()
+        split_rows(0)
+        column_start()
+        for g in range(2):
+            rows_start(g, owners - 1)
 
     @pl.when(inner == 1)
     def _():
-        for kind, c in relay_order(chunks):
-            if kind == "column":
-                column_wait(c, upper)
-                spread_rows(c)
+        for kind, o, c in relay_order(shares):
+            if kind == "plane":
+                add_gram(1, 0, owned)
+                plane_start()
+            elif kind == "column":
+                column_start()
+            elif kind == "rows":
+                rows_start(c, owners - 1 if owned else owners)
+            elif kind == "final":
+                near_copy(c, inward).wait_recv()
+                sum_copy(1, c, inward).wait_recv()
+                rows = rows_at(1, c, CHUNK)
+                whole[rows, :] = partial_ref[rows, :] + near[c] + landed[chunk_of(1, c)]
+                back_copy(1, c, inward).start()
+                back_copy(1, c, outward).start()
             elif kind == "inward" or kind == "outward":
-                half, to = (inward, toward_middle) if kind == "inward" else (outward, toward_end)
-                going = sum_copy(half, c, to)
+                going = sum_copy(o, c, inward if kind == "inward" else outward)
                 going.wait_recv()
-                rows = chunk_rows(half, c)
-                partial_ref[rows, :] = partial_ref[rows, :] + landed[half, c]
+                rows = rows_at(o, c, CHUNK)
+                partial_ref[rows, :] = partial_ref[rows, :] + landed[chunk_of(o, c)]
                 going.start()
             else:
-                half, to = (outward, toward_middle) if kind == "back_inward" else (inward, toward_end)
-                going = back_copy(half, c, to)
+                going = back_copy(o, c, inward if kind == "back_inward" else outward)
                 going.wait_recv()
                 going.start()
-        split_half(inward)
-        split_half(outward)
+        for o in range(n_light):
+            split_rows(o)
 
     def row_whole(g):
         others = groups[g][3].at[pl.ds(1, n_texel - 1)]
@@ -346,13 +393,6 @@
         work[index * height : (index + 1) * height, :size] = rows_first[index] / valid
 
     def finish_gram():
-        @pl.when(inner == 0)
-        def _():
-            for c in range(chunks):
-                back_copy(inward, c, toward_middle).wait_recv()
-
-            split_half(inward)
-
         row_whole(1).wait_recv()
         height = rows_rest.shape[1]
         rest = jnp.concatenate([rows_rest[index] for index in range(n_texel)], axis=0) / valid
@@ -361,7 +401,15 @@
         work[2 * quarter : 3 * quarter, 2 * quarter : size] = rest[quarter:, : 2 * quarter]
         work[3 * quarter :, 2 * quarter : size] = rest[quarter:, 2 * quarter :]
 
-    factor_inverse(work, finish_gram)
+    def finish_rows():
+        @pl.when(inner == 0)
+        def _():
+            for o in range(1, n_light):
+                for c in range(shares[o]):
+                    back_copy(o, c, inward).wait_recv()
+                split_rows(o)
+
+    factor_inverse(work, finish_gram, finish_rows)
     inverse = split(work[:, size:])
     half_ref[...] = product(inverse, (high[...], low[...])).astype(jnp.bfloat16)
     basis_out = pltpu.make_async_copy(basis_ref, basis_hbm, local_sems.at[0])
@@ -383,16 +431,15 @@
 
     @pl.when(inner == 0)
     def _():
-        all_sent(whole, back_send, outward)
-        for g in range(2):
-            sent = groups[g][1].at[pl.ds(0, n_light - 1)]
-            copy(sent, sent, column_send.at[g], column_recv.at[g, upper], (texel, lights[1])).wait_send()
+        all_sent(back_send, ends)
+        column_sent()
 
     @pl.when(inner == 1)
     def _():
-        for half in (inward, outward):
-            all_sent(partial_ref, sum_send, half)
-            all_sent(whole, back_send, half)
+        all_sent(sum_send, 2 * ends + owned)
+        all_sent(back_send, 2 * ends + 3 * owned)
+        if owned:
+            column_sent()
 
     for g in range(2):
         row_whole(g).wait_send()
@@ -497,7 +544,8 @@
     capacity, size = tex_feat.shape[0], sketch.shape[1]
     lights = light_feat.shape[0]
     block, step = capacity // 4, next(w for w in (256, 128) if lights % w == 0)
-    chunks, piece = capacity // 2 // CHUNK, size // n_texel
+    shares, _ = layout_of(capacity, n_light)
+    owners, piece = sum(1 for share in shares if share), size // n_texel
     first, rest = size // 4 // n_texel, size // 2 // n_texel
     width, bits = lights // 2, n_texel.bit_length() - 1
     vmem = pl.BlockSpec(memory_space=pltpu.VMEM)
@@ -524,7 +572,8 @@
             pltpu.VMEM((block, step), f32),
             pltpu.VMEM((block, step), f32),
             pltpu.VMEM((capacity, size), f32),
-            pltpu.VMEM((2, chunks, CHUNK, size), f32),
+            pltpu.VMEM((capacity // CHUNK, CHUNK, size), f32),
+            pltpu.VMEM((max(shares[1], 1), CHUNK, size), f32),
             pltpu.VMEM((capacity, size), f32),
             pltpu.VMEM((size, 2 * size), f32),
             pltpu.VMEM((size, size), f32),
@@ -532,11 +581,11 @@
             pltpu.VMEM((capacity, size), half),
             pltpu.VMEM((n_texel, first, size), f32), pltpu.VMEM((n_texel, rest, size), f32),
             pltpu.VMEM((n_texel, first, size), f32), pltpu.VMEM((n_texel, rest, size), f32),
-            pltpu.VMEM((2, first, size), f32), pltpu.VMEM((2, rest, size), f32),
+            pltpu.VMEM((owners, first, size), f32), pltpu.VMEM((owners, rest, size), f32),
             pltpu.VMEM((n_texel, first, size), f32), pltpu.VMEM((n_texel, rest, size), f32),
-            sems((2,)), sems((2,)), sems((2, chunks)),
+            sems, sems, sems((capacity // CHUNK,)), sems((max(shares[1], 1),)),
             sems((2,)), sems((2,)),
-            sems((2,)), sems((2, 2)),
+            sems((2,)), sems((2,)),
             sems((2,)), sems((2,)),
             sems((2,)), sems((2, n_texel - 1)),
             sems((5,)), sems((5,)),

time: 61 us -> 59.1 us (0.969)
  Pallas kernels: 60.1 us -> 58.1 us
    pallas_call x1, Pallas kernels: 59 us -> 57.1 us  [on_device(): pl.pallas_call(functools.partial(whole_step, n_texel, n_light), out_shape...]
where the time goes in v5:
time: 59.1 us; the launch traced here: 58.9 us
  Pallas kernels  58.1 us (98%)
  between operations  0.8 us (1%)
    pallas_call x1, Pallas kernels, on_device(): pl.pallas_call(functools.partial(whole_step, n_texel, n_light), out_shape...  57.1 us

profile of v5, /device:TPU:0, one launch (start us, length us, event | category | flops | bytes accessed | tf_op | source)
XLA Modules:
  0.0 58.9 jit_solution(9866692965704980835)
XLA Ops:
  0.6 57.1 %shard_map.59 = (f32[1024,256]{1,0:T(8,128)S(1)}, f32[32,1536]{1,0:T(8,128)S(1)}) custom-call(bf16[1024,512]{1,0:T(8,128)(2,1)} %tex_hbm.1, bf16[1536,512]{1,0:T(8,128)(2,1)} %feat_hbm.1, bf16[1536,256]{1,0:T(8,128)(2,1)} %sketch_hbm.1, s32[8]{0:T(128)} %counts_hbm.1), custom_call_target="tpu_custom_call" | custom-call | tf_op jit(solution)/shard_map/pallas_call | solution.py:555
  57.7 1.0 %shard_map.60 = (f32[1024,256]{1,0:T(8,128)}, f32[32,1536]{1,0:T(8,128)}) custom-call(f32[1024,256]{1,0:T(8,128)S(1)} %get-tuple-element.4.basis_ref, f32[32,1536]{1,0:T(8,128)S(1)} %get-tuple-element.5.coeffs_ref), custom_call_target="tpu_custom_call" | custom-call | tf_op jit(solution)/shard_map/pallas_call | solution.py:595

commit v6 on v5

--- a/solution.py
+++ b/solution.py
@@ -133,8 +133,8 @@
 
 
 def whole_step(
-    n_texel, n_light, tex_hbm, feat_hbm, sketch_hbm, counts_hbm, basis_hbm, coeffs_hbm,
-    tex_ref, feat_ref, sketch_ref, counts_ref, basis_ref, coeffs_ref,
+    n_texel, n_light, tex_hbm, feat_hbm, sketch_hbm, counts_hbm, basis_ref, coeffs_ref,
+    tex_ref, feat_ref, sketch_ref, counts_ref,
     tile_ref, half_ref, product_ref, held, arrived,
     logits_even, logits_odd, partial_ref,
     landed, near, whole, work, gram, high, low,
@@ -176,14 +176,16 @@
         pltpu.make_async_copy(tex_hbm.at[rows], tex_ref.at[rows], tex_sems.at[index])
         for index, (rows, _, _) in enumerate(turns)
     ]
+    feat_half = feat_ref.shape[0] // width // 2
     feat_copies = [
         pltpu.make_async_copy(
-            feat_hbm.at[pl.ds(c * width, width)], feat_ref.at[pl.ds(c * width, width)], local_sems.at[4]
+            feat_hbm.at[pl.ds(c * width, width)], feat_ref.at[pl.ds(c * width, width)],
+            local_sems.at[2 + c // feat_half],
         )
         for c in range(feat_ref.shape[0] // width)
     ]
-    sketch_copy = pltpu.make_async_copy(sketch_hbm, sketch_ref, local_sems.at[2])
-    counts_copy = pltpu.make_async_copy(counts_hbm, counts_ref, local_sems.at[3])
+    sketch_copy = pltpu.make_async_copy(sketch_hbm, sketch_ref, local_sems.at[0])
+    counts_copy = pltpu.make_async_copy(counts_hbm, counts_ref, local_sems.at[1])
     for going in tex_copies[:1] + feat_copies + [counts_copy, sketch_copy]:
         going.start()
     lights = [lax.rem(light + d, n_light) for d in range(n_light)]
@@ -228,7 +230,15 @@
         logits = (logits_even.at[pl.ds(0, height)], logits_odd.at[pl.ds(0, height)])
         count = feat_ref.shape[0] // width
 
+        def feat_wait(part):
+            rows = pl.ds(part * feat_half * width, feat_half * width)
+            pltpu.make_async_copy(feat_hbm.at[rows], feat_ref.at[rows], local_sems.at[2 + part]).wait()
+
         def product_of(c):
+            if turn == 0 and c == feat_half:
+                feat_wait(1)
+                for going in tex_copies[1:]:
+                    going.start()
             return lax.dot_general(
                 tex_ref[rows, :], feat_ref[c * width : (c + 1) * width, :], (((1,), (1,)), ((), ())),
                 preferred_element_type=jnp.float32,
@@ -236,9 +246,7 @@
 
         tex_copies[turn].wait()
         if turn == 0:
-            pltpu.make_async_copy(feat_hbm, feat_ref, local_sems.at[4]).wait()
-            for going in tex_copies[1:]:
-                going.start()
+            feat_wait(0)
         logits[0][...] = product_of(0)
         for c in range(count):
             if c + 1 < count:
@@ -412,19 +420,14 @@
     factor_inverse(work, finish_gram, finish_rows)
     inverse = split(work[:, size:])
     half_ref[...] = product(inverse, (high[...], low[...])).astype(jnp.bfloat16)
-    basis_out = pltpu.make_async_copy(basis_ref, basis_hbm, local_sems.at[0])
 
     def basis_rows(step):
         rows = slice(step * middle, (step + 1) * middle)
         basis_ref[rows, :] = product((high[rows, :], low[rows, :]), inverse)
-        if step == 1:
-            basis_out.start()
 
     scatter_sum(
         n_texel, half_ref, tile_ref, product_ref, coeffs_ref, valid, held, arrived, out_send, out_recv, basis_rows
     )
-    coeffs_out = pltpu.make_async_copy(coeffs_ref, coeffs_hbm, local_sems.at[1])
-    coeffs_out.start()
     for half in range(2):
         sent = held.at[half, pl.ds(0, n_texel - 1)]
         copy(sent, sent, out_send.at[half], out_recv.at[half, 0], (texels[1], light)).wait_send()
@@ -443,8 +446,6 @@
 
     for g in range(2):
         row_whole(g).wait_send()
-    basis_out.wait()
-    coeffs_out.wait()
 
 
 def halving_order(bits, last_first):
@@ -530,10 +531,12 @@
 
 
 def write_out(basis_ref, coeffs_ref, basis_out, coeffs_out, sems):
-    copies = [
-        pltpu.make_async_copy(basis_ref, basis_out, sems.at[0]),
-        pltpu.make_async_copy(coeffs_ref, coeffs_out, sems.at[1]),
-    ]
+    parts = sems.shape[0] - 1
+    height = basis_ref.shape[0] // parts
+    copies = [pltpu.make_async_copy(coeffs_ref, coeffs_out, sems.at[parts])]
+    for index in range(parts):
+        rows = pl.ds(index * height, height)
+        copies.append(pltpu.make_async_copy(basis_ref.at[rows], basis_out.at[rows], sems.at[index]))
     for going in copies:
         going.start()
     for going in copies:
@@ -556,14 +559,12 @@
         functools.partial(whole_step, n_texel, n_light),
         out_shape=(pltpu.VMEM((capacity, size), f32), pltpu.VMEM((piece, lights), f32)),
         in_specs=[anywhere] * 4,
-        out_specs=(anywhere, anywhere),
+        out_specs=(vmem, vmem),
         scratch_shapes=[
             pltpu.VMEM(tex_feat.shape, half),
             pltpu.VMEM(light_feat.shape, half),
             pltpu.VMEM(sketch.shape, half),
             pltpu.SMEM(row_counts.shape, jnp.int32),
-            pltpu.VMEM((capacity, size), f32),
-            pltpu.VMEM((piece, lights), f32),
             pltpu.VMEM((capacity, lights), half),
             pltpu.VMEM((size, capacity), half),
             pltpu.VMEM((size, lights), f32),
@@ -588,7 +589,7 @@
             sems((2,)), sems((2,)),
             sems((2,)), sems((2,)),
             sems((2,)), sems((2, n_texel - 1)),
-            sems((5,)), sems((5,)),
+            sems((4,)), sems((5,)),
         ],
         compiler_params=pltpu.CompilerParams(collective_id=1, has_side_effects=True),
     )(tex_feat, light_feat, sketch, row_counts)
@@ -597,7 +598,7 @@
         out_shape=(jax.ShapeDtypeStruct((capacity, size), f32), jax.ShapeDtypeStruct((piece, lights), f32)),
         in_specs=[vmem, vmem],
         out_specs=(pl.BlockSpec(memory_space=pl.ANY),) * 2,
-        scratch_shapes=[sems((2,))],
+        scratch_shapes=[sems((5,))],
     )(*(pltpu.with_memory_space_constraint(x, pltpu.VMEM) for x in (basis, coeffs)))
 
 

time: 59.1 us -> 58.8 us (level)
  no operation moved by 1% of the time
where the time goes in v6:
time: 58.8 us; the launch traced here: 58.6 us
  Pallas kernels  57.8 us (98%)
  between operations  0.8 us (1%)
    pallas_call x1, Pallas kernels, on_device(): pl.pallas_call(functools.partial(whole_step, n_texel, n_light), out_shape...  56.8 us

profile of v6, /device:TPU:0, one launch (start us, length us, event | category | flops | bytes accessed | tf_op | source)
XLA Modules:
  0.0 58.6 jit_solution(14045518820245212373)
XLA Ops:
  0.6 56.8 %shard_map.59 = (f32[1024,256]{1,0:T(8,128)S(1)}, f32[32,1536]{1,0:T(8,128)S(1)}) custom-call(bf16[1024,512]{1,0:T(8,128)(2,1)} %tex_hbm.1, bf16[1536,512]{1,0:T(8,128)(2,1)} %feat_hbm.1, bf16[1536,256]{1,0:T(8,128)(2,1)} %sketch_hbm.1, s32[8]{0:T(128)} %counts_hbm.1), custom_call_target="tpu_custom_call" | custom-call | tf_op jit(solution)/shard_map/pallas_call | solution.py:558
  57.4 1.1 %shard_map.60 = (f32[1024,256]{1,0:T(8,128)}, f32[32,1536]{1,0:T(8,128)}) custom-call(f32[1024,256]{1,0:T(8,128)S(1)} %get-tuple-element.4.basis_ref, f32[32,1536]{1,0:T(8,128)S(1)} %get-tuple-element.5.coeffs_ref), custom_call_target="tpu_custom_call" | custom-call | tf_op jit(solution)/shard_map/pallas_call | solution.py:596

commit v7 on v6

--- a/solution.py
+++ b/solution.py
@@ -212,7 +212,7 @@
         )
 
     def near_copy(c, to):
-        return copy(partial_ref.at[rows_at(1, c, CHUNK)], near.at[c], sum_send, near_recv.at[c], (texel, to))
+        return copy(partial_ref.at[rows_at(1, c, CHUNK)], near.at[c], sum_send, near_recv, (texel, to))
 
     def back_copy(o, c, to):
         rows = rows_at(o, c, CHUNK)
@@ -368,7 +368,8 @@
             elif kind == "rows":
                 rows_start(c, owners - 1 if owned else owners)
             elif kind == "final":
-                near_copy(c, inward).wait_recv()
+                if c == 0:
+                    copy(near, near, sum_send, near_recv, (texel, inward)).wait_recv()
                 sum_copy(1, c, inward).wait_recv()
                 rows = rows_at(1, c, CHUNK)
                 whole[rows, :] = partial_ref[rows, :] + near[c] + landed[chunk_of(1, c)]
@@ -511,8 +512,9 @@
                 copy.start()
                 used[half] += 1
                 flights[half][step, kept] = copy
-        if step < 2:
-            meanwhile(step)
+        if step == 1:
+            meanwhile(0)
+            meanwhile(1)
         if step:
             for half, order in enumerate(orders):
                 for key in [k for k in flights[half] if k[0] == step - 1]:
@@ -584,7 +586,7 @@
             pltpu.VMEM((n_texel, first, size), f32), pltpu.VMEM((n_texel, rest, size), f32),
             pltpu.VMEM((owners, first, size), f32), pltpu.VMEM((owners, rest, size), f32),
             pltpu.VMEM((n_texel, first, size), f32), pltpu.VMEM((n_texel, rest, size), f32),
-            sems, sems, sems((capacity // CHUNK,)), sems((max(shares[1], 1),)),
+            sems, sems, sems((capacity // CHUNK,)), sems,
             sems((2,)), sems((2,)),
             sems((2,)), sems((2,)),
             sems((2,)), sems((2,)),

time: 58.8 us -> 58.8 us (level)
  no operation moved by 1% of the time
where the time goes in v7:
time: 58.8 us; the launch traced here: 58.6 us
  Pallas kernels  57.8 us (98%)
  between operations  0.8 us (1%)
    pallas_call x1, Pallas kernels, on_device(): pl.pallas_call(functools.partial(whole_step, n_texel, n_light), out_shape...  56.7 us

profile of v7, /device:TPU:0, one launch (start us, length us, event | category | flops | bytes accessed | tf_op | source)
XLA Modules:
  0.0 58.6 jit_solution(18015770286879424744)
XLA Ops:
  0.6 56.7 %shard_map.59 = (f32[1024,256]{1,0:T(8,128)S(1)}, f32[32,1536]{1,0:T(8,128)S(1)}) custom-call(bf16[1024,512]{1,0:T(8,128)(2,1)} %tex_hbm.1, bf16[1536,512]{1,0:T(8,128)(2,1)} %feat_hbm.1, bf16[1536,256]{1,0:T(8,128)(2,1)} %sketch_hbm.1, s32[8]{0:T(128)} %counts_hbm.1), custom_call_target="tpu_custom_call" | custom-call | tf_op jit(solution)/shard_map/pallas_call | solution.py:560
  57.4 1.1 %shard_map.60 = (f32[1024,256]{1,0:T(8,128)}, f32[32,1536]{1,0:T(8,128)}) custom-call(f32[1024,256]{1,0:T(8,128)S(1)} %get-tuple-element.4.basis_ref, f32[32,1536]{1,0:T(8,128)S(1)} %get-tuple-element.5.coeffs_ref), custom_call_target="tpu_custom_call" | custom-call | tf_op jit(solution)/shard_map/pallas_call | solution.py:598
